TPU v7x, 256 devices: a whole 4x4x8 slice. The times are simulated.
256 devices in a mesh: inst: 4 (over z_hi), shard: 64 (over y, x, z_lo, core).
Axes of the slice: x: 4, y: 4, z: 8 (z_hi: 4, z_lo: 2; z = z_hi * 2 + z_lo), core: 2. Of those that a mesh axis runs over, the one named last changes fastest.
Arguments:
- master_old: float32 [4, 128, 65536], P('inst', 'shard'), may hold values from -3 to 3
- first_old: float32 [4, 128, 65536], P('inst', 'shard'), may hold values from -2 to 2
- second_old: float32 [4, 128, 65536], P('inst', 'shard'), may hold values from 0.01 to 1
- healthy: int32 [64], replicated, may hold values from 0 to 3
- slice_table: int32 [128], replicated, may hold values from 0 to 127, as said below
Outputs:
- master_new: float32 [4, 128, 65536], P('inst', 'shard')
- first_new: float32 [4, 128, 65536], P('inst', 'shard')
- second_new: float32 [4, 128, 65536], P('inst', 'shard')
- params_half: bfloat16 [4, 128, 65536], P('inst', 'shard')
- checksum: float32 [4, 2], P('inst')
Inputs may be any that keep to these rules, and one draw needn't show every extreme that they name: slice_table[k] = (k + slice_table[0]) mod 128 for every k, with slice_table[0] odd and at least 3.
All inputs are finite; a program needn't handle non-finite values.
Results may differ from a plain program's by a relative error of at most 0.001.
Values sent between devices are 32-bit elements; how exact they have to be, the bound alone decides.
A program may use at most 64 MiB of HBM per device.

v0:
```python
import jax
import jax.numpy as jnp
from jax import lax
from jax.sharding import PartitionSpec as P


def from_everyone(shard, axis):
    length = lax.axis_size(axis)
    return lax.all_to_all(
        jnp.broadcast_to(shard[None], (length, *shard.shape)), axis, 0, 0, tiled=True
    )


def over_copies(shard, axis):
    return from_everyone(shard, axis).sum(axis=0)


def in_order(parts, dim):
    lengths = list(parts.shape[1:])
    lengths[dim] *= parts.shape[0]
    return jnp.moveaxis(parts, 0, dim).reshape(lengths)


def gathered_copies(shard, axis, dim):
    parts = from_everyone(shard, axis)
    return in_order(parts, dim)


def side_by_side(arrays, axis, dim, along):
    ends, at = ([], 0)
    for a in arrays[:-1]:
        at += a.shape[along]
        ends.append(at)
    both = jnp.concatenate(arrays, axis=along)
    return tuple(jnp.split(gathered_copies(both, axis, dim), ends, axis=along))


def passed_along(value, axis, steps):
    count = lax.axis_size(axis)
    pairs = [(source, (source + steps) % count) for source in range(count)]
    return lax.ppermute(value, axis, pairs)


def from_root(shard, axis, root):
    return lax.dynamic_index_in_dim(lax.all_gather(shard, axis), root, 0, keepdims=False)


def position_keys(flat_rows, columns):
    residue = flat_rows * (columns % 101) % 101
    offsets = jnp.arange(columns, dtype=jnp.int32)
    cycled = (residue[:, None] + offsets[None, :]) % 101
    return (cycled * 37 % 101 + 1).astype(jnp.float32) / 101.0


def weighted(master, first_moment, second, flat_rows):
    weights = position_keys(flat_rows, master.shape[2])
    combined = master[0] + first_moment[0] + second[0]
    return jnp.stack([jnp.sum(combined * weights), jnp.sum(master[0] * weights)])


def grand_total(partial_value):
    return over_copies(partial_value, "shard")


def join_parts(pieces):
    return side_by_side((pieces[0], pieces[1], pieces[2]), "inst", 2, 0)


def reorder(arrays, rotation, owners):
    for bit_level in range((owners - 1).bit_length()):
        shifted = passed_along((arrays[0], arrays[1], arrays[2]), "shard", 1 << bit_level)
        chosen = rotation >> bit_level & 1 == 1
        arrays = tuple(
            (
                jnp.where(chosen, shifted_one, current)
                for shifted_one, current in zip(shifted, arrays)
            )
        )
    carried = passed_along((arrays[0][:, 1:2], arrays[1][:, 1:2], arrays[2][:, 1:2]), "shard", 1)
    return tuple(
        (
            jnp.concatenate([carried_one, current[:, 0:1]], axis=1)
            for carried_one, current in zip(carried, arrays)
        )
    )


def on_device(master_old, first_old, second_old, healthy, slice_table):
    source_index = lax.dynamic_index_in_dim(healthy, lax.axis_index("shard"), 0, keepdims=False)
    owners = lax.axis_size("shard")
    instances = lax.axis_size("inst")
    columns = master_old.shape[2]
    part_len = columns // instances
    normalizer = 1.0 / (2.0 * columns)
    rotation = slice_table[0] // 2
    master, first_moment, second = (
        from_root(master_old, "inst", source_index),
        from_root(first_old, "inst", source_index),
        from_root(second_old, "inst", source_index),
    )
    offset_start = lax.axis_index("inst") * part_len
    pieces = tuple(
        (
            lax.dynamic_slice_in_dim(stacked, offset_start, part_len, 2)
            for stacked in (master, first_moment, second)
        )
    )
    pieces = reorder(pieces, rotation, owners)
    master, first_moment, second = join_parts(pieces)
    new_rows = 2 * lax.axis_index("shard") + jnp.arange(2, dtype=jnp.int32)
    checksum = grand_total(weighted(master, first_moment, second, new_rows))
    checksum = jnp.reshape(checksum * normalizer, (1, 2))
    return (master, first_moment, second, master.astype(jnp.bfloat16), checksum)


def solution(mesh):
    placed = (
        P("inst", "shard", None),
        P("inst", "shard", None),
        P("inst", "shard", None),
        P(),
        P(),
    )
    return jax.shard_map(
        on_device,
        mesh=mesh,
        in_specs=placed,
        out_specs=(
            P("inst", "shard", None),
            P("inst", "shard", None),
            P("inst", "shard", None),
            P("inst", "shard", None),
            P("inst", None),
        ),
        check_vma=False,
    )
```

profile of v0, /device:TPU:1, one launch (start us, length us, event | category | flops | bytes accessed | tf_op | source)
XLA Modules:
  0.0 298.9 jit_solution(6419964372420753846)
XLA Ops:
  7.2 0.7 all-gather.7.cloned.1.call-update
  7.9 0.7 all-gather.9.cloned.1.call-update
  8.7 0.7 all-gather.11.cloned.1.call-update
  12.0 1.2 dynamic_slice.23
  15.2 48.9 %all-gather.7.cloned.1.call-done = f32[4,2,65536]{2,1,0:T(2,128)} async-done(((f32[1,2,65536]{2,1,0:T(2,128)}), f32[4,2,65536]{2,1,0:T(2,128)}) %all-gather.7.cloned.1.call-update) | async-done | bytes 2097168 | tf_op jit(solution)/shard_map/all_gather | solution.py:45
  64.1 1.1 constant_dynamic-slice_fusion.2
  65.2 2.3 collective-permute-start
  67.6 48.4 %all-gather.9.cloned.1.call-done = f32[4,2,65536]{2,1,0:T(2,128)} async-done(((f32[1,2,65536]{2,1,0:T(2,128)}), f32[4,2,65536]{2,1,0:T(2,128)}) %all-gather.9.cloned.1.call-update) | async-done | bytes 2097168 | tf_op jit(solution)/shard_map/all_gather | solution.py:45
  115.9 1.1 constant_dynamic-slice_fusion.1
  117.0 2.3 collective-permute-start.7
  119.4 48.4 %all-gather.11.cloned.1.call-done = f32[4,2,65536]{2,1,0:T(2,128)} async-done(((f32[1,2,65536]{2,1,0:T(2,128)}), f32[4,2,65536]{2,1,0:T(2,128)}) %all-gather.11.cloned.1.call-update) | async-done | bytes 2097168 | tf_op jit(solution)/shard_map/all_gather | solution.py:45
  167.7 1.1 constant_dynamic-slice_fusion
  168.8 2.3 collective-permute-start.14
  171.2 1.1 broadcast_select_fusion.2
  172.3 1.0 collective-permute-start.1
  173.3 1.1 broadcast_select_fusion.1
  174.4 2.0 collective-permute-start.8
  176.4 1.1 broadcast_select_fusion
  177.5 0.5 collective-permute-start.15
  178.1 3.9 %collective-permute-done.1 = f32[1,2,16384]{2,1,0:T(2,128)S(1)} collective-permute-done((f32[1,2,16384]{2,1,0:T(2,128)S(1)}, f32[1,2,16384]{2,1,0:T(2,128)S(1)}, u32[]{:S(2)}, u32[]{:S(2)}) %collective-permute-start.1) | collective-permute-done | bytes 131104 | tf_op jit(solution)/shard_map/ppermute | solution.py:41
  182.1 0.1 collective-permute-start.2
  182.2 2.6 collective-permute-done.8
  184.9 0.1 collective-permute-start.9
  185.0 1.1 collective-permute-done.15
  186.1 0.1 collective-permute-start.16
  186.2 5.9 %collective-permute-done.2 = f32[1,2,16384]{2,1,0:T(2,128)S(1)} collective-permute-done((f32[1,2,16384]{2,1,0:T(2,128)S(1)}, f32[1,2,16384]{2,1,0:T(2,128)S(1)}, u32[]{:S(2)}, u32[]{:S(2)}) %collective-permute-start.2) | collective-permute-done | bytes 131104 | tf_op jit(solution)/shard_map/ppermute | solution.py:41
  192.2 0.1 collective-permute-start.3
  192.3 2.6 collective-permute-done.9
  195.0 0.1 collective-permute-start.10
  195.1 1.0 collective-permute-done.16
  196.2 0.1 collective-permute-start.17
  196.3 4.1 %collective-permute-done.3 = f32[1,2,16384]{2,1,0:T(2,128)S(1)} collective-permute-done((f32[1,2,16384]{2,1,0:T(2,128)S(1)}, f32[1,2,16384]{2,1,0:T(2,128)S(1)}, u32[]{:S(2)}, u32[]{:S(2)}) %collective-permute-start.3) | collective-permute-done | bytes 131104 | tf_op jit(solution)/shard_map/ppermute | solution.py:41
  200.4 0.1 collective-permute-start.4
  200.5 2.6 collective-permute-done.10
  203.2 0.3 collective-permute-start.11
  203.5 2.4 collective-permute-done.17
  206.1 3.6 %collective-permute-done.4 = f32[1,2,16384]{2,1,0:T(2,128)S(1)} collective-permute-done((f32[1,2,16384]{2,1,0:T(2,128)S(1)}, f32[1,2,16384]{2,1,0:T(2,128)S(1)}, u32[]{:S(2)}, u32[]{:S(2)}) %collective-permute-start.4) | collective-permute-done | bytes 131104 | tf_op jit(solution)/shard_map/ppermute | solution.py:41
  209.8 0.1 collective-permute-start.5
  209.9 2.1 collective-permute-done.11
  212.1 0.9 collective-permute-start.12
  213.0 2.5 collective-permute-done.18
  215.6 0.1 collective-permute-start.19
  215.7 1.2 collective-permute-done.5
  217.0 0.1 fusion.5
  217.1 1.7 collective-permute-start.6
  218.7 1.0 collective-permute-done.12
  219.8 0.1 fusion.6
  219.9 0.3 collective-permute-start.13
  220.1 2.6 collective-permute-done.19
  222.8 0.1 fusion.7
  223.0 0.6 collective-permute-done.13
  223.6 1.7 collective-permute-done.20
  225.2 0.4 maximum_maximum_fusion
  225.6 1.7 broadcast_in_dim.4
  227.4 6.3 %all-to-all-start = ((f32[4,3,2,16384]{3,2,1,0:T(2,128)}), f32[4,3,2,16384]{3,2,1,0:T(2,128)S(1)}, u32[]{:S(2)}, u32[]{:S(2)}) async-start(f32[4,3,2,16384]{3,2,1,0:T(2,128)} %broadcast_in_dim.4), calls=%async_computation | async-start | bytes 3145728 | tf_op jit(solution)/shard_map/all_to_all | solution.py:9
  233.7 36.5 %all-to-all-done = f32[4,3,2,16384]{3,2,1,0:T(2,128)S(1)} async-done(((f32[4,3,2,16384]{3,2,1,0:T(2,128)}), f32[4,3,2,16384]{3,2,1,0:T(2,128)S(1)}, u32[]{:S(2)}, u32[]{:S(2)}) %all-to-all-start) | async-done | bytes 1572896 | tf_op jit(solution)/shard_map/all_to_all | solution.py:9
  270.2 5.0 %multiply_reduce_fusion.1 = (f32[]{:T(128)}, f32[]{:T(128)}, f32[1,2,4,16384]{3,1,0,2:T(2,128)}, f32[1,2,4,16384]{3,1,0,2:T(2,128)}, f32[1,2,4,16384]{3,1,0,2:T(2,128)S(1)}) fusion(s32[4,16384]{1,0:T(4,128)S(1)} %multiply_add_fusion, s32[2]{0:T(128)S(1)} %and_select_fusion.2, f32[3,2,4,16384]{3,1,0,2:T(2,128)S(1)} %bitcast.11), kind=kLoop, calls=%fused_computation.8 | loop fusion | flops 3014654 | bytes 3407888 | tf_op jit(solution)/shard_map/reduce_sum | solution.py:58
  275.2 1.4 pad_maximum_fusion
  276.6 0.6 broadcast_in_dim.5
  277.2 6.8 %all-to-all-start.1 = ((f32[64,1,2]{2,1,0:T(1,128)}), f32[64,1,2]{2,1,0:T(1,128)S(1)}, u32[]{:S(2)}, u32[]{:S(2)}) async-start(f32[64,1,2]{2,1,0:T(1,128)} %broadcast_in_dim.5), calls=%async_computation.1 | async-start | bytes 65536 | tf_op jit(solution)/shard_map/all_to_all | solution.py:9
  284.0 0.9 convert_element_type.22
  284.8 6.9 %all-to-all-done.1 = f32[64,1,2]{2,1,0:T(1,128)S(1)} async-done(((f32[64,1,2]{2,1,0:T(1,128)}), f32[64,1,2]{2,1,0:T(1,128)S(1)}, u32[]{:S(2)}, u32[]{:S(2)}) %all-to-all-start.1) | async-done | bytes 544 | tf_op jit(solution)/shard_map/all_to_all | solution.py:9
  291.7 0.1 reduce_sum.29
  291.8 0.5 multiply_bitcast_fusion
  (28 shorter events, 1.4 us)
Async XLA Ops:
  7.2 56.9 %all-gather.7.cloned.1.call-start = ((), (), s32[]{:S(2)}) async-start(), calls=%async_computation.2 | async-start | bytes 2621440 | tf_op jit(solution)/shard_map/all_gather | solution.py:45
  7.9 108.0 %all-gather.9.cloned.1.call-start = ((), (), s32[]{:S(2)}) async-start(), calls=%async_computation.3 | async-start | bytes 2621440 | tf_op jit(solution)/shard_map/all_gather | solution.py:45
  8.6 159.1 %all-gather.11.cloned.1.call-start = ((), (), s32[]{:S(2)}) async-start(), calls=%async_computation.4 | async-start | bytes 2621440 | tf_op jit(solution)/shard_map/all_gather | solution.py:45
  65.2 106.0 %collective-permute-start = (f32[1,2,16384]{2,1,0:T(2,128)S(1)}, f32[1,2,16384]{2,1,0:T(2,128)S(1)}, u32[]{:S(2)}, u32[]{:S(2)}) collective-permute-start(f32[1,2,16384]{2,1,0:T(2,128)S(1)} %constant_dynamic-slice_fusion.2), channel_id=1, source_target_pairs={{0,1},{1,2},{2,3},{3,4},{4,5},{5,6},{6,7},{7,8},{8,9},{9,10},{10,1... | collective-permute-start | bytes 393224 | tf_op jit(solution)/shard_map/ppermute | solution.py:41
  117.0 56.3 %collective-permute-start.7 = (f32[1,2,16384]{2,1,0:T(2,128)S(1)}, f32[1,2,16384]{2,1,0:T(2,128)S(1)}, u32[]{:S(2)}, u32[]{:S(2)}) collective-permute-start(f32[1,2,16384]{2,1,0:T(2,128)S(1)} %constant_dynamic-slice_fusion.1), channel_id=1, source_target_pairs={{0,1},{1,2},{2,3},{3,4},{4,5},{5,6},{6,7},{7,8},{8,9},{9,10},{10,1... | collective-permute-start | bytes 393224 | tf_op jit(solution)/shard_map/ppermute | solution.py:41
  168.8 7.6 %collective-permute-start.14 = (f32[1,2,16384]{2,1,0:T(2,128)S(1)}, f32[1,2,16384]{2,1,0:T(2,128)S(1)}, u32[]{:S(2)}, u32[]{:S(2)}) collective-permute-start(f32[1,2,16384]{2,1,0:T(2,128)S(1)} %constant_dynamic-slice_fusion), channel_id=1, source_target_pairs={{0,1},{1,2},{2,3},{3,4},{4,5},{5,6},{6,7},{7,8},{8,9},{9,10},{10,1... | collective-permute-start | bytes 393224 | tf_op jit(solution)/shard_map/ppermute | solution.py:41
  172.3 9.7 %collective-permute-start.1 = (f32[1,2,16384]{2,1,0:T(2,128)S(1)}, f32[1,2,16384]{2,1,0:T(2,128)S(1)}, u32[]{:S(2)}, u32[]{:S(2)}) collective-permute-start(f32[1,2,16384]{2,1,0:T(2,128)S(1)} %broadcast_select_fusion.2), channel_id=1, source_target_pairs={{0,2},{1,3},{2,4},{3,5},{4,6},{5,7},{6,8},{7,9},{8,10},{9,11},{10,... | collective-permute-start | bytes 393224 | tf_op jit(solution)/shard_map/ppermute | solution.py:41
  174.4 10.4 %collective-permute-start.8 = (f32[1,2,16384]{2,1,0:T(2,128)S(1)}, f32[1,2,16384]{2,1,0:T(2,128)S(1)}, u32[]{:S(2)}, u32[]{:S(2)}) collective-permute-start(f32[1,2,16384]{2,1,0:T(2,128)S(1)} %broadcast_select_fusion.1), channel_id=1, source_target_pairs={{0,2},{1,3},{2,4},{3,5},{4,6},{5,7},{6,8},{7,9},{8,10},{9,11},{10,... | collective-permute-start | bytes 393224 | tf_op jit(solution)/shard_map/ppermute | solution.py:41
  177.5 8.5 %collective-permute-start.15 = (f32[1,2,16384]{2,1,0:T(2,128)S(1)}, f32[1,2,16384]{2,1,0:T(2,128)S(1)}, u32[]{:S(2)}, u32[]{:S(2)}) collective-permute-start(f32[1,2,16384]{2,1,0:T(2,128)S(1)} %broadcast_select_fusion), channel_id=1, source_target_pairs={{0,2},{1,3},{2,4},{3,5},{4,6},{5,7},{6,8},{7,9},{8,10},{9,11},{10,... | collective-permute-start | bytes 393224 | tf_op jit(solution)/shard_map/ppermute | solution.py:41
  182.1 10.0 %collective-permute-start.2 = (f32[1,2,16384]{2,1,0:T(2,128)S(1)}, f32[1,2,16384]{2,1,0:T(2,128)S(1)}, u32[]{:S(2)}, u32[]{:S(2)}) collective-permute-start(f32[1,2,16384]{2,1,0:T(2,128)S(1)} %broadcast_select_fusion.5), channel_id=1, source_target_pairs={{0,4},{1,5},{2,6},{3,7},{4,8},{5,9},{6,10},{7,11},{8,12},{9,13},{1... | collective-permute-start | bytes 393224 | tf_op jit(solution)/shard_map/ppermute | solution.py:41
  184.9 10.0 %collective-permute-start.9 = (f32[1,2,16384]{2,1,0:T(2,128)S(1)}, f32[1,2,16384]{2,1,0:T(2,128)S(1)}, u32[]{:S(2)}, u32[]{:S(2)}) collective-permute-start(f32[1,2,16384]{2,1,0:T(2,128)S(1)} %broadcast_select_fusion.4), channel_id=1, source_target_pairs={{0,4},{1,5},{2,6},{3,7},{4,8},{5,9},{6,10},{7,11},{8,12},{9,13},{1... | collective-permute-start | bytes 393224 | tf_op jit(solution)/shard_map/ppermute | solution.py:41
  186.1 10.0 %collective-permute-start.16 = (f32[1,2,16384]{2,1,0:T(2,128)S(1)}, f32[1,2,16384]{2,1,0:T(2,128)S(1)}, u32[]{:S(2)}, u32[]{:S(2)}) collective-permute-start(f32[1,2,16384]{2,1,0:T(2,128)S(1)} %broadcast_select_fusion.3), channel_id=1, source_target_pairs={{0,4},{1,5},{2,6},{3,7},{4,8},{5,9},{6,10},{7,11},{8,12},{9,13},{1... | collective-permute-start | bytes 393224 | tf_op jit(solution)/shard_map/ppermute | solution.py:41
  192.2 8.2 %collective-permute-start.3 = (f32[1,2,16384]{2,1,0:T(2,128)S(1)}, f32[1,2,16384]{2,1,0:T(2,128)S(1)}, u32[]{:S(2)}, u32[]{:S(2)}) collective-permute-start(f32[1,2,16384]{2,1,0:T(2,128)S(1)} %broadcast_select_fusion.8), channel_id=1, source_target_pairs={{0,8},{1,9},{2,10},{3,11},{4,12},{5,13},{6,14},{7,15},{8,16},{9,17... | collective-permute-start | bytes 393224 | tf_op jit(solution)/shard_map/ppermute | solution.py:41
  195.0 8.2 %collective-permute-start.10 = (f32[1,2,16384]{2,1,0:T(2,128)S(1)}, f32[1,2,16384]{2,1,0:T(2,128)S(1)}, u32[]{:S(2)}, u32[]{:S(2)}) collective-permute-start(f32[1,2,16384]{2,1,0:T(2,128)S(1)} %broadcast_select_fusion.7), channel_id=1, source_target_pairs={{0,8},{1,9},{2,10},{3,11},{4,12},{5,13},{6,14},{7,15},{8,16},{9,17... | collective-permute-start | bytes 393224 | tf_op jit(solution)/shard_map/ppermute | solution.py:41
  196.2 9.7 %collective-permute-start.17 = (f32[1,2,16384]{2,1,0:T(2,128)S(1)}, f32[1,2,16384]{2,1,0:T(2,128)S(1)}, u32[]{:S(2)}, u32[]{:S(2)}) collective-permute-start(f32[1,2,16384]{2,1,0:T(2,128)S(1)} %broadcast_select_fusion.6), channel_id=1, source_target_pairs={{0,8},{1,9},{2,10},{3,11},{4,12},{5,13},{6,14},{7,15},{8,16},{9,17... | collective-permute-start | bytes 393224 | tf_op jit(solution)/shard_map/ppermute | solution.py:41
  200.4 9.3 %collective-permute-start.4 = (f32[1,2,16384]{2,1,0:T(2,128)S(1)}, f32[1,2,16384]{2,1,0:T(2,128)S(1)}, u32[]{:S(2)}, u32[]{:S(2)}) collective-permute-start(f32[1,2,16384]{2,1,0:T(2,128)S(1)} %broadcast_select_fusion.11), channel_id=1, source_target_pairs={{0,16},{1,17},{2,18},{3,19},{4,20},{5,21},{6,22},{7,23},{8,24},{9,... | collective-permute-start | bytes 393224 | tf_op jit(solution)/shard_map/ppermute | solution.py:41
  203.2 8.8 %collective-permute-start.11 = (f32[1,2,16384]{2,1,0:T(2,128)S(1)}, f32[1,2,16384]{2,1,0:T(2,128)S(1)}, u32[]{:S(2)}, u32[]{:S(2)}) collective-permute-start(f32[1,2,16384]{2,1,0:T(2,128)S(1)} %broadcast_select_fusion.10), channel_id=1, source_target_pairs={{0,16},{1,17},{2,18},{3,19},{4,20},{5,21},{6,22},{7,23},{8,24},{9,... | collective-permute-start | bytes 393224 | tf_op jit(solution)/shard_map/ppermute | solution.py:41
  206.0 9.5 %collective-permute-start.18 = (f32[1,2,16384]{2,1,0:T(2,128)S(1)}, f32[1,2,16384]{2,1,0:T(2,128)S(1)}, u32[]{:S(2)}, u32[]{:S(2)}) collective-permute-start(f32[1,2,16384]{2,1,0:T(2,128)S(1)} %broadcast_select_fusion.9), channel_id=1, source_target_pairs={{0,16},{1,17},{2,18},{3,19},{4,20},{5,21},{6,22},{7,23},{8,24},{9,... | collective-permute-start | bytes 393224 | tf_op jit(solution)/shard_map/ppermute | solution.py:41
  209.8 7.1 %collective-permute-start.5 = (f32[1,2,16384]{2,1,0:T(2,128)S(1)}, f32[1,2,16384]{2,1,0:T(2,128)S(1)}, u32[]{:S(2)}, u32[]{:S(2)}) collective-permute-start(f32[1,2,16384]{2,1,0:T(2,128)S(1)} %broadcast_select_fusion.14), channel_id=1, source_target_pairs={{0,32},{1,33},{2,34},{3,35},{4,36},{5,37},{6,38},{7,39},{8,40},{9,... | collective-permute-start | bytes 393224 | tf_op jit(solution)/shard_map/ppermute | solution.py:41
  212.1 7.6 %collective-permute-start.12 = (f32[1,2,16384]{2,1,0:T(2,128)S(1)}, f32[1,2,16384]{2,1,0:T(2,128)S(1)}, u32[]{:S(2)}, u32[]{:S(2)}) collective-permute-start(f32[1,2,16384]{2,1,0:T(2,128)S(1)} %broadcast_select_fusion.13), channel_id=1, source_target_pairs={{0,32},{1,33},{2,34},{3,35},{4,36},{5,37},{6,38},{7,39},{8,40},{9,... | collective-permute-start | bytes 393224 | tf_op jit(solution)/shard_map/ppermute | solution.py:41
  215.6 7.1 %collective-permute-start.19 = (f32[1,2,16384]{2,1,0:T(2,128)S(1)}, f32[1,2,16384]{2,1,0:T(2,128)S(1)}, u32[]{:S(2)}, u32[]{:S(2)}) collective-permute-start(f32[1,2,16384]{2,1,0:T(2,128)S(1)} %broadcast_select_fusion.12), channel_id=1, source_target_pairs={{0,32},{1,33},{2,34},{3,35},{4,36},{5,37},{6,38},{7,39},{8,40},{9,... | collective-permute-start | bytes 393224 | tf_op jit(solution)/shard_map/ppermute | solution.py:41
  217.1 5.9 %collective-permute-start.6 = (f32[1,1,16384]{2,1,0:T(1,128)S(1)}, f32[1,1,16384]{2,1,0:T(1,128)S(1)}, u32[]{:S(2)}, u32[]{:S(2)}) collective-permute-start(f32[1,1,16384]{2,1,0:T(1,128)S(1)} %get-tuple-element.10), channel_id=1, source_target_pairs={{0,1},{1,2},{2,3},{3,4},{4,5},{5,6},{6,7},{7,8},{8,9},{9,10},{10,1... | collective-permute-start | bytes 196616 | tf_op jit(solution)/shard_map/ppermute | solution.py:41
  219.9 3.7 %collective-permute-start.13 = (f32[1,1,16384]{2,1,0:T(1,128)S(1)}, f32[1,1,16384]{2,1,0:T(1,128)S(1)}, u32[]{:S(2)}, u32[]{:S(2)}) collective-permute-start(f32[1,1,16384]{2,1,0:T(1,128)S(1)} %get-tuple-element.12), channel_id=1, source_target_pairs={{0,1},{1,2},{2,3},{3,4},{4,5},{5,6},{6,7},{7,8},{8,9},{9,10},{10,1... | collective-permute-start | bytes 196616 | tf_op jit(solution)/shard_map/ppermute | solution.py:41
  222.9 2.4 collective-permute-start.20
  227.4 42.9 %all-to-all-start = ((f32[4,3,2,16384]{3,2,1,0:T(2,128)}), f32[4,3,2,16384]{3,2,1,0:T(2,128)S(1)}, u32[]{:S(2)}, u32[]{:S(2)}) async-start(f32[4,3,2,16384]{3,2,1,0:T(2,128)} %broadcast_in_dim.4), calls=%async_computation | async-start | bytes 3145728 | tf_op jit(solution)/shard_map/all_to_all | solution.py:9
  275.2 17.2 %copy-start = (f32[1,2,4,16384]{3,1,0,2:T(2,128)}, f32[1,2,4,16384]{3,1,0,2:T(2,128)S(1)}, u32[]{:S(2)}) copy-start(f32[1,2,4,16384]{3,1,0,2:T(2,128)S(1)} %get-tuple-element.9) | copy-start | bytes 1572868
  277.2 14.6 %all-to-all-start.1 = ((f32[64,1,2]{2,1,0:T(1,128)}), f32[64,1,2]{2,1,0:T(1,128)S(1)}, u32[]{:S(2)}, u32[]{:S(2)}) async-start(f32[64,1,2]{2,1,0:T(1,128)} %broadcast_in_dim.5), calls=%async_computation.1 | async-start | bytes 65536 | tf_op jit(solution)/shard_map/all_to_all | solution.py:9
Sparse Core Ops, SparseCore 0:
  9.8 54.2 all-gather.6
  65.9 49.9 all-gather.8
  117.7 49.9 all-gather.10
where the time goes:
time: 299 us
  waiting for transfers between devices  233 us (78%)
  starting transfers between devices  27.8 us (9%)
  between operations  18.6 us (6%)
  other arithmetic  12.6 us (4%)
  local copies, waits for them, and re-layouts  7.22 us (2%)
    all_gather x3, waiting for transfers between devices, from_root(): lax.all_gather(shard, axis)  146 us
    all_to_all x2, waiting for transfers between devices, from_everyone(): lax.all_to_all(jnp.broadcast_to(shard[None], (length, *shard.shape)), axi...  43.4 us
    ppermute x21, waiting for transfers between devices, passed_along(): return lax.ppermute(value, axis, pairs)  41.6 us
    ppermute x21, starting transfers between devices, passed_along(): return lax.ppermute(value, axis, pairs)  14.6 us
    all_to_all x2, starting transfers between devices, from_everyone(): lax.all_to_all(jnp.broadcast_to(shard[None], (length, *shard.shape)), axi...  13 us
  transfers between devices with their start and end apart: 26, of which 22 were waited for; matrix products, arithmetic and copies ran while one was open for 3% of the time, Pallas kernels for 0%

commit v1 on v0

v1 whole, which is shorter than its diff:
```python
import functools

import jax
import jax.numpy as jnp
from jax import lax
from jax.experimental import pallas as pl
from jax.experimental.pallas import tpu as pltpu
from jax.sharding import PartitionSpec as P

MESH = pl.DeviceIdType.MESH
KINDS = 3
GROUP = 16


def to_lines(shard, pieces):
    rows, columns = shard.shape[1:]
    lanes = shard.reshape(rows, columns // 128, 128)
    return lanes.transpose(1, 0, 2).reshape(pieces, columns * rows // (128 * pieces), 128)


def from_lines(lines, rows, columns):
    lanes = lines.reshape(columns // 128, rows, 128)
    return lanes.transpose(1, 0, 2).reshape(1, rows, columns)


def kernel(n_inst, n_shard, healthy, table, master, first, second, out, sums_out,
           own, got, staged, final, part, part_got, total, total_got,
           load_sem, spread_send, spread_recv, deal_send, deal_recv,
           part_send, part_recv, total_send, total_recv, store_sem):
    n_all = n_inst * n_shard
    inst = lax.axis_index("inst")
    shard = lax.axis_index("shard")
    me = inst * n_shard + shard
    height = own.shape[2]

    loads = [
        pltpu.make_async_copy(source, own.at[:, kind], load_sem.at[kind])
        for kind, source in enumerate((master, first, second))
    ]
    for load in loads:
        load.start()
    for load in loads:
        load.wait()

    def peer(step):
        to_inst = lax.rem(inst + lax.rem(step, n_inst), n_inst)
        to_shard = lax.rem(shard + step // n_inst, n_shard)
        return to_inst, to_shard

    def spread(step, carry):
        to_inst, to_shard = peer(step)
        pltpu.make_async_remote_copy(
            src_ref=own.at[to_inst * n_shard + to_shard],
            dst_ref=got.at[me],
            send_sem=spread_send,
            recv_sem=spread_recv,
            device_id=(to_inst, to_shard),
            device_id_type=MESH,
        ).start()
        return carry

    lax.fori_loop(1, n_all, spread, 0)
    got[me] = own[me]

    block = 16
    shape = (block, height, 128)
    line = lax.broadcasted_iota(jnp.int32, shape, 1)
    lane = lax.broadcasted_iota(jnp.int32, shape, 2)
    piece = lax.broadcasted_iota(jnp.int32, shape, 0)
    row = line & 1
    slice_0, slice_1 = table[2 * shard], table[2 * shard + 1]
    row_base = jnp.where(row == 0, slice_0 * 88, slice_1 * 88)
    base = row_base + piece * (64 * height) + (line >> 1) * 128 + lane

    def mod_101(x):
        return x - ((x * 10382) >> 20) * 101

    def weigh(step, carry):
        all_sum, master_sum = carry
        at = pl.ds(step * block, block)
        key = mod_101(mod_101(base + step * (block * 64 * height)) * 37) + 1
        key = key.astype(jnp.float32)
        m = own[at, 0]
        term = m * key
        rest = (own[at, 1] + own[at, 2]) * key
        return all_sum + (term + rest), master_sum + term

    zero = jnp.zeros(shape, jnp.float32)
    all_sum, master_sum = lax.fori_loop(0, n_all // block, weigh, (zero, zero))
    mine = healthy[shard] == inst
    both = jnp.stack([all_sum.sum(axis=0).sum(axis=0), master_sum.sum(axis=0).sum(axis=0)])
    part[...] = jnp.where(mine, both, 0.0)

    per_y = n_shard // 4
    y, low = shard // per_y, lax.rem(shard, per_y)
    group_at = inst * 4 + y

    def share_part(step, carry):
        to = lax.rem(group_at + step, GROUP)
        pltpu.make_async_remote_copy(
            src_ref=part,
            dst_ref=part_got.at[group_at],
            send_sem=part_send,
            recv_sem=part_recv,
            device_id=(to // 4, lax.rem(to, 4) * per_y + low),
            device_id_type=MESH,
        ).start()
        return carry

    lax.fori_loop(1, GROUP, share_part, 0)
    part_got[group_at] = part[...]

    def wait_for(source, target, send_sem, recv_sem):
        return pltpu.make_async_remote_copy(
            src_ref=source,
            dst_ref=target,
            send_sem=send_sem,
            recv_sem=recv_sem,
            device_id=(inst, shard),
            device_id_type=MESH,
        )

    most = pl.ds(0, n_all - 1)
    spread_all = wait_for(own.at[most], got.at[most], spread_send, spread_recv)
    spread_all.wait_recv()

    rotation = table[0] >> 1

    def stage(new, carry):
        low_from = (new - rotation - 1) & (n_shard - 1)
        high_from = (new - rotation) & (n_shard - 1)
        low = got[healthy[low_from] * n_shard + low_from]
        high = got[healthy[high_from] * n_shard + high_from]
        lines = []
        for pair in range(0, height, 2):
            lines += [low[:, pair + 1:pair + 2], high[:, pair:pair + 1]]
        staged[new] = jnp.concatenate(lines, axis=1)
        return carry

    lax.fori_loop(0, n_shard, stage, 0)

    def deal(step, carry):
        to_inst, to_shard = peer(step)
        pltpu.make_async_remote_copy(
            src_ref=staged.at[to_shard],
            dst_ref=final.at[:, me],
            send_sem=deal_send,
            recv_sem=deal_recv,
            device_id=(to_inst, to_shard),
            device_id_type=MESH,
        ).start()
        return carry

    lax.fori_loop(1, n_all, deal, 0)
    final[:, me] = staged[shard]

    few = pl.ds(0, GROUP - 1)
    parts_all = wait_for(part_got.at[few], part_got.at[few], part_send, part_recv)
    parts_all.wait_recv()
    total[...] = part_got[...].sum(axis=0)

    def share_total(step, carry):
        to = lax.rem(low + step, GROUP)
        pltpu.make_async_remote_copy(
            src_ref=total,
            dst_ref=total_got.at[low],
            send_sem=total_send,
            recv_sem=total_recv,
            device_id=(inst, y * per_y + to),
            device_id_type=MESH,
        ).start()
        return carry

    lax.fori_loop(1, GROUP, share_total, 0)
    total_got[low] = total[...]
    totals_all = wait_for(total_got.at[few], total_got.at[few], total_send, total_recv)
    totals_all.wait_recv()
    sums_out[...] = total_got[...].sum(axis=0)

    deal_all = wait_for(own.at[most], final.at[:, most], deal_send, deal_recv)
    deal_all.wait_recv()
    store = pltpu.make_async_copy(final, out, store_sem)
    store.start()
    spread_all.wait_send()
    parts_all.wait_send()
    totals_all.wait_send()
    deal_all.wait_send()
    store.wait()


def on_device(n_inst, n_shard, master_old, first_old, second_old, healthy, slice_table):
    rows, columns = master_old.shape[1:]
    n_all = n_inst * n_shard
    height = rows * columns // (128 * n_all)
    lines = [to_lines(a, n_all) for a in (master_old, first_old, second_old)]
    anywhere = pl.BlockSpec(memory_space=pl.ANY)
    vmem = pl.BlockSpec(memory_space=pltpu.VMEM)
    smem = pl.BlockSpec(memory_space=pltpu.SMEM)
    dma = pltpu.SemaphoreType.DMA
    out, sums = pl.pallas_call(
        functools.partial(kernel, n_inst, n_shard),
        out_shape=(
            jax.ShapeDtypeStruct((KINDS, n_all, height, 128), jnp.float32),
            jax.ShapeDtypeStruct((2, 128), jnp.float32),
        ),
        in_specs=[smem, smem, anywhere, anywhere, anywhere],
        out_specs=(anywhere, vmem),
        scratch_shapes=[
            pltpu.VMEM((n_all, KINDS, height, 128), jnp.float32),
            pltpu.VMEM((n_all, KINDS, height, 128), jnp.float32),
            pltpu.VMEM((n_shard, KINDS, height, 128), jnp.float32),
            pltpu.VMEM((KINDS, n_all, height, 128), jnp.float32),
            pltpu.VMEM((2, 128), jnp.float32),
            pltpu.VMEM((GROUP, 2, 128), jnp.float32),
            pltpu.VMEM((2, 128), jnp.float32),
            pltpu.VMEM((GROUP, 2, 128), jnp.float32),
            dma((KINDS,)),
            dma, dma, dma, dma, dma, dma, dma, dma, dma,
        ],
        compiler_params=pltpu.CompilerParams(has_side_effects=True),
    )(healthy, slice_table, *lines)
    master, first_moment, second = (from_lines(out[k], rows, columns) for k in range(KINDS))
    checksum = jnp.sum(sums, axis=1).reshape(1, 2) * (1.0 / (101.0 * 2.0 * columns))
    return master, first_moment, second, master.astype(jnp.bfloat16), checksum


def solution(mesh):
    per_slice = P("inst", "shard", None)
    return jax.shard_map(
        functools.partial(on_device, mesh.shape["inst"], mesh.shape["shard"]),
        mesh=mesh,
        in_specs=(per_slice, per_slice, per_slice, P(), P()),
        out_specs=(per_slice, per_slice, per_slice, per_slice, P("inst", None)),
        check_vma=False,
    )
```

time: 299 us -> 103 us (0.34)
  waiting for transfers between devices: 233 us -> 0 us
  Pallas kernels: 0 us -> 97.9 us
  starting transfers between devices: 27.8 us -> 0 us
  between operations: 18.6 us -> 0.65 us
  other arithmetic: 12.6 us -> 1.56 us
  local copies, waits for them, and re-layouts: 7.22 us -> 2.43 us
    all_gather x3 -> x0, waiting for transfers between devices: 146 us -> none  [from_root(): lax.all_gather(shard, axis)]
    pallas_call x0 -> x1, Pallas kernels: none -> 97.9 us  [on_device(): pl.pallas_call(functools.partial(kernel, n_inst, n_shard), out_shape=(jax...]
    all_to_all x2 -> x0, waiting for transfers between devices: 43.4 us -> none  [from_everyone(): lax.all_to_all(jnp.broadcast_to(shard[None], (length, *shard.shape)), axi...]
    ppermute x21 -> x0, waiting for transfers between devices: 41.6 us -> none  [passed_along(): return lax.ppermute(value, axis, pairs)]
    ppermute x21 -> x0, starting transfers between devices: 14.6 us -> none  [passed_along(): return lax.ppermute(value, axis, pairs)]
    all_to_all x2 -> x0, starting transfers between devices: 13 us -> none  [from_everyone(): lax.all_to_all(jnp.broadcast_to(shard[None], (length, *shard.shape)), axi...]
    reduce_sum x2 -> x1, other arithmetic: 5.05 us -> 0.12 us  [on_device(): jnp.sum(sums, axis=1).reshape(1, 2) * (1.0 / (101.0 * 2.0 * columns))]
    dynamic_slice x4 -> x0, local copies, waits for them, and re-layouts: 4.55 us -> none  [the longest x3 3.3 us: on_device(): lax.dynamic_slice_in_dim(stacked, offset_start, part_len, 2)]
  transfers between devices with their start and end apart: 26 -> 0, of which waited for: 22 -> 0; matrix products, arithmetic and copies ran while one was open for 3% -> 0% of each run, Pallas kernels for 0% -> 0%
where the time goes in v1:
time: 103 us
  Pallas kernels  97.9 us (95%)
  local copies, waits for them, and re-layouts  2.43 us (2%)
  other arithmetic  1.56 us (2%)
    pallas_call x1, Pallas kernels, on_device(): pl.pallas_call(functools.partial(kernel, n_inst, n_shard), out_shape=(jax...  97.9 us
    slice x1, local copies, waits for them, and re-layouts, on_device(): out[k]  2.43 us

profile of v1, /device:TPU:1, one launch (start us, length us, event | category | flops | bytes accessed | tf_op | source)
XLA Modules:
  0.0 102.6 jit_solution(11118689006082104912)
XLA Ops:
  0.6 97.9 %shard_map.92 = (f32[3,256,4,128]{3,2,1,0:T(4,128)}, f32[2,128]{1,0:T(2,128)}) custom-call(s32[64]{0:T(128)} %healthy.1, s32[128]{0:T(128)} %table.1, f32[256,4,128]{2,1,0:T(4,128)} %bitcast.34, f32[256,4,128]{2,1,0:T(4,128)} %bitcast.35, f32[256,4,128]{2,1,0:T(4,128)} %bitcast.36), custom_call_target="tpu_custom_call" | custom-call | tf_op jit(solution)/shard_map/pallas_call | solution.py:200
  98.6 0.0 copy-start.1
  98.6 2.4 %fusion = (f32[1,256,4,128]{3,2,1,0:T(4,128)}, f32[1,256,4,128]{3,2,1,0:T(4,128)}, f32[1,256,4,128]{3,2,1,0:T(4,128)S(1)}) fusion(f32[3,256,4,128]{3,2,1,0:T(4,128)} %get-tuple-element.7), kind=kLoop, calls=%fused_computation.1 | loop fusion | bytes 3145728 | tf_op jit(solution)/shard_map/slice | solution.py:222
  101.0 0.0 copy-start
  101.0 0.0 copy-done.1
  101.0 0.1 reduce_sum.9
  101.1 0.6 multiply_bitcast_fusion
  101.7 0.9 convert_element_type.11
  102.6 0.0 copy-done
Async XLA Ops:
  98.6 2.4 %copy-start.1 = (f32[2,128]{1,0:T(2,128)S(1)}, f32[2,128]{1,0:T(2,128)}, u32[]{:S(2)}) copy-start(f32[2,128]{1,0:T(2,128)} %get-tuple-element.8) | copy-start | bytes 3076
  101.0 1.6 %copy-start = (f32[1,256,4,128]{3,2,1,0:T(4,128)}, f32[1,256,4,128]{3,2,1,0:T(4,128)S(1)}, u32[]{:S(2)}) copy-start(f32[1,256,4,128]{3,2,1,0:T(4,128)S(1)} %get-tuple-element.11) | copy-start | bytes 1572868

commit v2 on v0

v2 whole, which is shorter than its diff:
```python
import functools

import jax
import jax.numpy as jnp
from jax import lax
from jax.experimental import pallas as pl
from jax.experimental.pallas import tpu as pltpu
from jax.sharding import PartitionSpec as P

MESH = pl.DeviceIdType.MESH
KINDS = 3
CHUNKS = 2
SIDE = 8


def to_pieces(shard, pieces):
    rows, columns = shard.shape[1:]
    lines = shard.reshape(rows, columns // 128, 128).transpose(1, 0, 2)
    return lines.reshape(*pieces, rows * columns // (128 * CHUNKS * pieces[1] * pieces[2] * 2), 128)


def from_pieces(pieces, rows, columns):
    lines = pieces.reshape(columns // 128, rows, 128)
    return lines.transpose(1, 0, 2).reshape(1, rows, columns)


def mod_101(x):
    return x - ((x * 10382) >> 20) * 101


def kernel(n_inst, n_shard, healthy, table, master, first, second, out, sums_out,
           own, relayed, mixed, staged, final, part, part_got, row, row_got, total, total_got,
           load_sem, relay_send, relay_recv, spread_send, spread_recv,
           deal_send, deal_recv, near_recv, far_send, far_recv,
           part_send, part_recv, row_send, row_recv, total_send, total_recv, store_sem, *got):
    inst = lax.axis_index("inst")
    shard = lax.axis_index("shard")
    pairs = n_shard // 2
    pair, core = shard // 2, lax.rem(shard, 2)
    height = own.shape[5]
    after = lax.rem(inst + 1, n_inst)
    across = lax.rem(inst + 2, n_inst)
    before = lax.rem(inst + 3, n_inst)

    def copy(source, target, send_sem, recv_sem, to_inst, to_shard):
        return pltpu.make_async_remote_copy(
            src_ref=source,
            dst_ref=target,
            send_sem=send_sem,
            recv_sem=recv_sem,
            device_id=(to_inst, to_shard),
            device_id_type=MESH,
        )

    def waiting(target, send_sem, recv_sem):
        return copy(target, target, send_sem, recv_sem, inst, shard)

    loads = [
        pltpu.make_async_copy(source, own.at[:, :, :, :, kind], load_sem.at[kind])
        for kind, source in enumerate((master, first, second))
    ]
    for load in loads:
        load.start()

    barrier = pltpu.get_barrier_semaphore()

    def greet(step, carry):
        to_shard = lax.rem(shard + step, n_shard)
        for to_inst in (after, before, inst):
            pl.semaphore_signal(barrier, inc=1, device_id=(to_inst, to_shard), device_id_type=MESH)
        return carry

    for to_inst in (after, across, before):
        pl.semaphore_signal(barrier, inc=1, device_id=(to_inst, shard), device_id_type=MESH)
    lax.fori_loop(1, n_shard, greet, 0)

    for load in loads:
        load.wait()

    block = (1, 1, 8, 2)
    shape = (*block, height, 128)
    at_pair = lax.broadcasted_iota(jnp.int32, shape, 2)
    at_core = lax.broadcasted_iota(jnp.int32, shape, 3)
    line = lax.broadcasted_iota(jnp.int32, shape, 4)
    lane = lax.broadcasted_iota(jnp.int32, shape, 5)
    slice_0, slice_1 = table[2 * shard], table[2 * shard + 1]
    row_base = jnp.where((line & 1) == 0, slice_0 * 88, slice_1 * 88)
    width = 64 * height
    base = row_base + (at_pair * 2 + at_core) * width + (line >> 1) * 128 + lane
    blocks = pairs // 8

    def weigh(step, carry):
        all_sum, master_sum = carry
        chunk = step // (n_inst * blocks)
        of_inst = lax.rem(step // blocks, n_inst)
        at = (pl.ds(chunk, 1), pl.ds(of_inst, 1), pl.ds(lax.rem(step, blocks) * 8, 8))
        key = mod_101(mod_101(base + step * (16 * width)) * 37) + 1
        key = key.astype(jnp.float32)
        m = own[at[0], at[1], at[2], :, 0]
        term = m * key
        rest = (own[at[0], at[1], at[2], :, 1] + own[at[0], at[1], at[2], :, 2]) * key
        return all_sum + (term + rest), master_sum + term

    zero = jnp.zeros(shape, jnp.float32)
    sums = lax.fori_loop(0, CHUNKS * n_inst * blocks, weigh, (zero, zero))
    mine = healthy[shard] == inst
    both = jnp.stack([s.reshape(16 * height, 128).sum(axis=0) for s in sums])
    part[...] = jnp.where(mine, both, 0.0)

    pl.semaphore_wait(barrier, 3 * n_shard)

    for to_inst in (after, across, before):
        copy(part, part_got.at[inst], part_send, part_recv, to_inst, shard).start()
    part_got[inst] = part[...]

    sides = ((after, 0), (before, 1))
    for chunk in range(CHUNKS):
        for to_inst, side in sides:
            copy(
                own.at[chunk, across, :, side], relayed.at[chunk, side],
                relay_send.at[chunk, side], relay_recv.at[chunk, side], to_inst, shard,
            ).start()

    def spread_to(chunk, source, slot, to_inst, to_shard):
        copy(
            source, got[chunk].at[slot * n_shard + shard],
            spread_send.at[chunk], spread_recv.at[chunk], to_inst, to_shard,
        ).start()

    def spread_own(chunk):
        partner = 1 - core
        spread_to(chunk, own.at[chunk, inst, pair, partner], 0, inst, pair * 2 + partner)
        got[chunk][shard] = own[chunk, inst, pair, core]

        def spread(step, carry):
            to = lax.rem(pair + step, pairs)
            spread_to(chunk, own.at[chunk, after, to, 1], 1, after, to * 2 + 1)
            spread_to(chunk, own.at[chunk, before, to, 0], 2, before, to * 2)

            @pl.when(step > 0)
            def _():
                spread_to(chunk, own.at[chunk, inst, to, 0], 0, inst, to * 2)
                spread_to(chunk, own.at[chunk, inst, to, 1], 0, inst, to * 2 + 1)

            return carry

        lax.fori_loop(0, pairs, spread, 0)

    def spread_mixed(chunk):
        of_mine = healthy[shard]
        for (to_inst, side), from_inst in zip(sides, (before, after)):
            waiting(relayed.at[chunk, side], relay_send.at[chunk, side], relay_recv.at[chunk, side]).wait_recv()

            def mix(step, carry):
                at = pl.ds(step * 4, 4)
                mixed[chunk, side, at] = jnp.where(
                    of_mine == from_inst, relayed[chunk, side, at], own[chunk, to_inst, at, side]
                )
                return carry

            lax.fori_loop(0, pairs // 4, mix, 0)

        def spread(step, carry):
            to = lax.rem(pair + step, pairs)
            spread_to(chunk, mixed.at[chunk, 0, to], 1, after, to * 2)
            spread_to(chunk, mixed.at[chunk, 1, to], 2, before, to * 2 + 1)
            return carry

        lax.fori_loop(0, pairs, spread, 0)

    for chunk in range(CHUNKS):
        spread_own(chunk)

    some = pl.ds(0, n_inst - 1)
    waiting(part_got.at[some], part_send, part_recv).wait()
    row[...] = part_got[...].sum(axis=0)
    side_at, place = shard // SIDE, lax.rem(shard, SIDE)

    def share_row(step, carry):
        to = lax.rem(place + step, SIDE)
        copy(row, row_got.at[place], row_send, row_recv, inst, side_at * SIDE + to).start()
        return carry

    lax.fori_loop(1, SIDE, share_row, 0)
    row_got[place] = row[...]

    for chunk in range(CHUNKS):
        spread_mixed(chunk)

    rotation = table[0] >> 1
    nearly = pl.ds(0, 3 * n_shard - 1)

    def held(chunk, owner):
        turn = (healthy[owner] - inst) & 3
        slot = jnp.where(turn == 0, 0, jnp.where(turn == 3, 1, jnp.where(turn == 1, 2, 1 + core)))
        return got[chunk][slot * n_shard + owner]

    def deal(chunk):
        waiting(got[chunk].at[nearly], spread_send.at[chunk], spread_recv.at[chunk]).wait_recv()

        def stage(new, carry):
            low = held(chunk, (new - rotation - 1) & (n_shard - 1))
            high = held(chunk, (new - rotation) & (n_shard - 1))
            lines = []
            for at in range(0, height, 2):
                lines += [low[:, at + 1:at + 2], high[:, at:at + 1]]
            staged[chunk, new] = jnp.concatenate(lines, axis=1)
            return carry

        lax.fori_loop(0, n_shard, stage, 0)
        near = lax.rem(inst + 3 + 2 * core, n_inst)
        other = lax.rem(inst + 1 + 2 * core, n_inst)
        place_there = final.at[:, chunk, inst, pair, core]

        def deal_near(step, carry):
            to = lax.rem(shard + step, n_shard)
            copy(staged.at[chunk, to], place_there, deal_send.at[chunk], near_recv.at[chunk, core], near, to).start()
            return carry

        def deal_rest(step, carry):
            to = lax.rem(shard + step, n_shard)
            copy(staged.at[chunk, to], place_there, deal_send.at[chunk], deal_recv.at[chunk], other, to).start()

            @pl.when(step > 0)
            def _():
                copy(staged.at[chunk, to], place_there, deal_send.at[chunk], deal_recv.at[chunk], inst, to).start()

            return carry

        lax.fori_loop(0, n_shard, deal_near, 0)
        lax.fori_loop(0, n_shard, deal_rest, 0)
        final[:, chunk, inst, pair, core] = staged[chunk, shard]

    def pass_on(chunk):
        for side, from_inst, to_inst in ((0, after, before), (1, before, after)):
            there = final.at[:, chunk, from_inst, :, side]
            waiting(there, deal_send.at[chunk], near_recv.at[chunk, side]).wait_recv()
            copy(there, there, far_send.at[chunk, side], far_recv.at[chunk, side], to_inst, shard).start()

    for chunk in range(CHUNKS):
        deal(chunk)
        if chunk == 0:
            few = pl.ds(0, SIDE - 1)
            waiting(row_got.at[few], row_send, row_recv).wait()
            total[...] = row_got[...].sum(axis=0)

            def share_total(step, carry):
                to = lax.rem(side_at + step, SIDE)
                copy(total, total_got.at[side_at], total_send, total_recv, inst, to * SIDE + place).start()
                return carry

            lax.fori_loop(1, SIDE, share_total, 0)
            total_got[side_at] = total[...]
    for chunk in range(CHUNKS):
        pass_on(chunk)

    waiting(total_got.at[pl.ds(0, SIDE - 1)], total_send, total_recv).wait()
    sums_out[...] = total_got[...].sum(axis=0)

    rest = pl.ds(0, 2 * n_shard - 1)
    for chunk in range(CHUNKS):
        waiting(got[chunk].at[rest], deal_send.at[chunk], deal_recv.at[chunk]).wait_recv()
        for side in range(2):
            waiting(
                final.at[:, chunk, across, :, side], far_send.at[chunk, side], far_recv.at[chunk, side]
            ).wait_recv()
        pltpu.make_async_copy(final.at[:, chunk], out.at[:, chunk], store_sem.at[chunk]).start()
    for chunk in range(CHUNKS):
        waiting(got[chunk].at[nearly], spread_send.at[chunk], spread_recv.at[chunk]).wait_send()
        waiting(got[chunk].at[nearly], deal_send.at[chunk], deal_recv.at[chunk]).wait_send()
        for side in range(2):
            waiting(relayed.at[chunk, side], relay_send.at[chunk, side], relay_recv.at[chunk, side]).wait_send()
            waiting(
                final.at[:, chunk, across, :, side], far_send.at[chunk, side], far_recv.at[chunk, side]
            ).wait_send()
        pltpu.make_async_copy(final.at[:, chunk], out.at[:, chunk], store_sem.at[chunk]).wait()


def on_device(n_inst, n_shard, master_old, first_old, second_old, healthy, slice_table):
    rows, columns = master_old.shape[1:]
    pairs = n_shard // 2
    pieces = (CHUNKS, n_inst, pairs, 2)
    arrays = [to_pieces(a, pieces) for a in (master_old, first_old, second_old)]
    tile = arrays[0].shape[4:]
    anywhere = pl.BlockSpec(memory_space=pl.ANY)
    vmem = pl.BlockSpec(memory_space=pltpu.VMEM)
    smem = pl.BlockSpec(memory_space=pltpu.SMEM)
    dma = pltpu.SemaphoreType.DMA

    def buffer(*shape):
        return pltpu.VMEM((*shape, *tile), jnp.float32)

    def sums(*shape):
        return pltpu.VMEM((*shape, 2, 128), jnp.float32)

    out, checks = pl.pallas_call(
        functools.partial(kernel, n_inst, n_shard),
        out_shape=(
            jax.ShapeDtypeStruct((KINDS, *pieces, *tile), jnp.float32),
            jax.ShapeDtypeStruct((2, 128), jnp.float32),
        ),
        in_specs=[smem, smem, anywhere, anywhere, anywhere],
        out_specs=(anywhere, vmem),
        scratch_shapes=[
            buffer(*pieces, KINDS),
            buffer(CHUNKS, 2, pairs, KINDS),
            buffer(CHUNKS, 2, pairs, KINDS),
            buffer(CHUNKS, n_shard, KINDS),
            buffer(KINDS, *pieces),
            sums(), sums(n_inst), sums(), sums(SIDE), sums(), sums(SIDE),
            dma((KINDS,)),
            dma((CHUNKS, 2)), dma((CHUNKS, 2)),
            dma((CHUNKS,)), dma((CHUNKS,)),
            dma((CHUNKS,)), dma((CHUNKS,)), dma((CHUNKS, 2)),
            dma((CHUNKS, 2)), dma((CHUNKS, 2)),
            dma, dma, dma, dma, dma, dma,
            dma((CHUNKS,)),
            *[buffer(3 * n_shard, KINDS) for _ in range(CHUNKS)],
        ],
        compiler_params=pltpu.CompilerParams(collective_id=0, has_side_effects=True),
    )(healthy, slice_table, *arrays)
    master, first_moment, second = (from_pieces(out[k], rows, columns) for k in range(KINDS))
    checksum = jnp.sum(checks, axis=1).reshape(1, 2) * (1.0 / (101.0 * 2.0 * columns))
    return master, first_moment, second, master.astype(jnp.bfloat16), checksum


def solution(mesh):
    per_slice = P("inst", "shard", None)
    return jax.shard_map(
        functools.partial(on_device, mesh.shape["inst"], mesh.shape["shard"]),
        mesh=mesh,
        in_specs=(per_slice, per_slice, per_slice, P(), P()),
        out_specs=(per_slice, per_slice, per_slice, per_slice, P("inst", None)),
        check_vma=False,
    )
```

time: 299 us -> 86.6 us (0.29)
  waiting for transfers between devices: 233 us -> 0 us
  Pallas kernels: 0 us -> 81.2 us
  starting transfers between devices: 27.8 us -> 0 us
  between operations: 18.6 us -> 0.65 us
  other arithmetic: 12.6 us -> 1.56 us
  local copies, waits for them, and re-layouts: 7.22 us -> 3.06 us
    all_gather x3 -> x0, waiting for transfers between devices: 146 us -> none  [from_root(): lax.all_gather(shard, axis)]
    pallas_call x0 -> x1, Pallas kernels: none -> 81.2 us  [on_device(): pl.pallas_call(functools.partial(kernel, n_inst, n_shard), out_shape=(jax...]
    all_to_all x2 -> x0, waiting for transfers between devices: 43.4 us -> none  [from_everyone(): lax.all_to_all(jnp.broadcast_to(shard[None], (length, *shard.shape)), axi...]
    ppermute x21 -> x0, waiting for transfers between devices: 41.6 us -> none  [passed_along(): return lax.ppermute(value, axis, pairs)]
    ppermute x21 -> x0, starting transfers between devices: 14.6 us -> none  [passed_along(): return lax.ppermute(value, axis, pairs)]
    all_to_all x2 -> x0, starting transfers between devices: 13 us -> none  [from_everyone(): lax.all_to_all(jnp.broadcast_to(shard[None], (length, *shard.shape)), axi...]
    reduce_sum x2 -> x1, other arithmetic: 5.05 us -> 0.12 us  [on_device(): jnp.sum(checks, axis=1).reshape(1, 2) * (1.0 / (101.0 * 2.0 * columns))]
    dynamic_slice x4 -> x0, local copies, waits for them, and re-layouts: 4.55 us -> none  [the longest x3 3.3 us: on_device(): lax.dynamic_slice_in_dim(stacked, offset_start, part_len, 2)]
  transfers between devices with their start and end apart: 26 -> 0, of which waited for: 22 -> 0; matrix products, arithmetic and copies ran while one was open for 3% -> 0% of each run, Pallas kernels for 0% -> 0%
where the time goes in v2:
time: 86.6 us; the launch traced here: 86.5 us
  Pallas kernels  81.2 us (94%)
  local copies, waits for them, and re-layouts  3.06 us (4%)
  other arithmetic  1.56 us (2%)
    pallas_call x1, Pallas kernels, on_device(): pl.pallas_call(functools.partial(kernel, n_inst, n_shard), out_shape=(jax...  81.2 us
    slice x1, local copies, waits for them, and re-layouts, on_device(): out[k]  3.06 us

profile of v2, /device:TPU:1, one launch (start us, length us, event | category | flops | bytes accessed | tf_op | source)
XLA Modules:
  0.0 86.5 jit_solution(3618942571442873233)
XLA Ops:
  0.6 81.2 %shard_map.92 = (f32[3,2,4,32,2,2,128]{6,5,4,3,2,1,0:T(2,128)}, f32[2,128]{1,0:T(2,128)}) custom-call(s32[64]{0:T(128)} %healthy.1, s32[128]{0:T(128)} %table.1, f32[2,4,32,2,2,128]{5,4,3,2,1,0:T(2,128)} %bitcast.34, f32[2,4,32,2,2,128]{5,4,3,2,1,0:T(2,128)} %bitcast.35, f32[2,4,32,2,2,128]{5,4,3,2,1,0:T(2,128)} %bitcast.36), custom_call_target="tpu_custom_call" | custom-call | tf_op jit(solution)/shard_map/pallas_call | solution.py:296
  81.8 0.0 copy-start.1
  81.9 3.1 %fusion = (f32[1,2,4,32,2,2,128]{6,5,4,3,2,1,0:T(2,128)}, f32[1,2,4,32,2,2,128]{6,5,4,3,2,1,0:T(2,128)}, f32[1,2,4,32,2,2,128]{6,5,4,3,2,1,0:T(2,128)S(1)}) fusion(f32[3,2,4,32,2,2,128]{6,5,4,3,2,1,0:T(2,128)} %get-tuple-element.7), kind=kLoop, calls=%fused_computation.1 | loop fusion | bytes 3145728 | tf_op jit(solution)/shard_map/slice | solution.py:322
  84.9 0.0 copy-start
  84.9 0.0 copy-done.1
  84.9 0.1 reduce_sum.9
  85.0 0.6 multiply_bitcast_fusion
  85.6 0.9 %convert_element_type.11 = bf16[1,2,65536]{2,1,0:T(2,128)(2,1)} convert(f32[1,2,65536]{2,1,0:T(2,128)S(1)} %bitcast.32) | non-fusion elementwise | flops 131072 | bytes 786432 | tf_op jit(solution)/shard_map/convert_element_type | solution.py:324
  86.5 0.0 copy-done
Async XLA Ops:
  81.8 3.1 %copy-start.1 = (f32[2,128]{1,0:T(2,128)S(1)}, f32[2,128]{1,0:T(2,128)}, u32[]{:S(2)}) copy-start(f32[2,128]{1,0:T(2,128)} %get-tuple-element.8) | copy-start | bytes 3076
  84.9 1.6 %copy-start = (f32[1,2,4,32,2,2,128]{6,5,4,3,2,1,0:T(2,128)}, f32[1,2,4,32,2,2,128]{6,5,4,3,2,1,0:T(2,128)S(1)}, u32[]{:S(2)}) copy-start(f32[1,2,4,32,2,2,128]{6,5,4,3,2,1,0:T(2,128)S(1)} %get-tuple-element.11) | copy-start | bytes 1572868

commit v3 on v2

v3 whole, which is shorter than its diff:
```python
import functools
import math

import jax
import jax.numpy as jnp
from jax import lax
from jax.experimental import pallas as pl
from jax.experimental.pallas import tpu as pltpu
from jax.sharding import PartitionSpec as P

MESH = pl.DeviceIdType.MESH
KINDS = 3
CHUNKS = 2
SIDE = 8


def to_pieces(shard, pieces):
    rows, columns = shard.shape[1:]
    lines = shard.reshape(rows, columns // 128, 128).transpose(1, 0, 2)
    return lines.reshape(*pieces, rows * columns // (128 * math.prod(pieces)), 128)


def from_pieces(pieces, rows, columns):
    lines = pieces.reshape(columns // 128, rows, 128)
    return lines.transpose(1, 0, 2).reshape(1, rows, columns)


def mod_101(x):
    return x - ((x * 10382) >> 20) * 101


def kernel(n_inst, n_shard, healthy, table, master, first, second, out, sums_out,
           own, cross_in, cross_out, level_in, level_out, staged, final,
           part, part_got, row, row_got, total, total_got,
           load_sem, relay_send, relay_recv, spread_send, spread_recv,
           deal_send, deal_recv, pass_recv, far_send, far_recv,
           part_send, part_recv, row_send, row_recv, total_send, total_recv, store_sem, *got):
    inst = lax.axis_index("inst")
    shard = lax.axis_index("shard")
    spots = n_shard // 4
    spot, level, core = shard // 4, lax.rem(shard // 2, 2), lax.rem(shard, 2)
    flip = 1 - level
    height = own.shape[6]
    after = lax.rem(inst + 1, n_inst)
    across = lax.rem(inst + 2, n_inst)
    before = lax.rem(inst + 3, n_inst)
    near = lax.rem(inst + 3 + 2 * level, n_inst)
    far = lax.rem(inst + 1 + 2 * level, n_inst)

    def copy(source, target, send_sem, recv_sem, to_inst, to_shard):
        return pltpu.make_async_remote_copy(
            src_ref=source,
            dst_ref=target,
            send_sem=send_sem,
            recv_sem=recv_sem,
            device_id=(to_inst, to_shard),
            device_id_type=MESH,
        )

    def waiting(target, send_sem, recv_sem):
        return copy(target, target, send_sem, recv_sem, inst, shard)

    loads = [
        pltpu.make_async_copy(source, own.at[:, :, :, :, :, kind], load_sem.at[kind])
        for kind, source in enumerate((master, first, second))
    ]
    for load in loads:
        load.start()

    barrier = pltpu.get_barrier_semaphore()

    def greet(to_inst, to_shard):
        pl.semaphore_signal(barrier, inc=1, device_id=(to_inst, to_shard), device_id_type=MESH)

    def greet_spot(step, carry):
        to = lax.rem(spot + step, spots) * 4
        for to_core in range(2):
            greet(near, to + 2 * flip + to_core)
            greet(inst, to + 2 * flip + to_core)
            greet(after, to + 2 * level + to_core)
            greet(before, to + 2 * level + to_core)

        @pl.when(step > 0)
        def _():
            for to_core in range(2):
                greet(inst, to + 2 * level + to_core)

        return carry

    lax.fori_loop(0, spots, greet_spot, 0)
    greet(inst, spot * 4 + 2 * level + 1 - core)
    greet(across, shard)

    for load in loads:
        load.wait()

    shape = (1, 1, 4, 2, 2, height, 128)
    at_spot = lax.broadcasted_iota(jnp.int32, shape, 2)
    at_level = lax.broadcasted_iota(jnp.int32, shape, 3)
    at_core = lax.broadcasted_iota(jnp.int32, shape, 4)
    line = lax.broadcasted_iota(jnp.int32, shape, 5)
    lane = lax.broadcasted_iota(jnp.int32, shape, 6)
    slice_0, slice_1 = table[2 * shard], table[2 * shard + 1]
    row_base = jnp.where((line & 1) == 0, slice_0 * 88, slice_1 * 88)
    width = 64 * height
    base = row_base + (at_spot * 4 + at_level * 2 + at_core) * width + (line >> 1) * 128 + lane
    blocks = spots // 4

    def weigh(step, carry):
        all_sum, master_sum = carry
        chunk = step // (n_inst * blocks)
        of_inst = lax.rem(step // blocks, n_inst)
        at = pl.ds(lax.rem(step, blocks) * 4, 4)
        key = mod_101(mod_101(base + step * (16 * width)) * 37) + 1
        key = key.astype(jnp.float32)
        m, f, s = (own[pl.ds(chunk, 1), pl.ds(of_inst, 1), at, :, :, kind] for kind in range(KINDS))
        term = m * key
        return all_sum + (term + (f + s) * key), master_sum + term

    zero = jnp.zeros(shape, jnp.float32)
    sums = lax.fori_loop(0, CHUNKS * n_inst * blocks, weigh, (zero, zero))
    of_mine = healthy[shard]
    both = jnp.stack([s.reshape(16 * height, 128).sum(axis=0) for s in sums])
    part[...] = jnp.where(of_mine == inst, both, 0.0)

    pl.semaphore_wait(barrier, 5 * n_shard // 2)

    for to_inst in (after, across, before):
        copy(part, part_got.at[inst], part_send, part_recv, to_inst, shard).start()
    part_got[inst] = part[...]

    def relays(chunk):
        return (
            (own.at[chunk, far, :, flip], cross_in.at[chunk, 0], 0, far),
            (own.at[chunk, across, :, flip], cross_in.at[chunk, 1], 1, near),
            (own.at[chunk, across, :, level, 0], level_in.at[chunk, 0], 2, after),
            (own.at[chunk, across, :, level, 1], level_in.at[chunk, 1], 3, before),
        )

    def relay(chunk):
        for source, target, which, to_inst in relays(chunk):
            copy(source, target, relay_send.at[chunk, which], relay_recv.at[chunk, which], to_inst, shard).start()

    def spread_to(chunk, source, slot, to_inst, to_shard):
        copy(
            source, got[chunk].at[slot * n_shard + shard],
            spread_send.at[chunk], spread_recv.at[chunk], to_inst, to_shard,
        ).start()

    def spread_own(chunk):
        got[chunk][shard] = own[chunk, inst, spot, level, core]
        partner = 1 - core
        spread_to(chunk, own.at[chunk, inst, spot, level, partner], 0, inst, spot * 4 + 2 * level + partner)

        def spread(step, carry):
            to = lax.rem(spot + step, spots)
            to_shard = to * 4 + 2 * level
            spread_to(chunk, own.at[chunk, after, to, level, 1], 1, after, to_shard + 1)
            spread_to(chunk, own.at[chunk, before, to, level, 0], 2, before, to_shard)

            @pl.when(step > 0)
            def _():
                spread_to(chunk, own.at[chunk, inst, to, level, 0], 0, inst, to_shard)
                spread_to(chunk, own.at[chunk, inst, to, level, 1], 0, inst, to_shard + 1)

            return carry

        lax.fori_loop(0, spots, spread, 0)

    def mix(chunk):
        for _, target, which, _ in relays(chunk):
            waiting(target, relay_send.at[chunk, which], relay_recv.at[chunk, which]).wait_recv()

        def at_spots(step, carry):
            at = pl.ds(step * 4, 4)
            for which, from_inst, to_inst in ((0, near, inst), (1, far, near)):
                cross_out[chunk, which, at] = jnp.where(
                    of_mine == from_inst, cross_in[chunk, which, at], own[chunk, to_inst, at, flip]
                )
            for which, from_inst, to_inst in ((0, before, after), (1, after, before)):
                level_out[chunk, which, at] = jnp.where(
                    of_mine == from_inst, level_in[chunk, which, at], own[chunk, to_inst, at, level, which]
                )
            return carry

        lax.fori_loop(0, spots // 4, at_spots, 0)

    def spread_mixed(chunk):
        def spread(step, carry):
            to = lax.rem(spot + step, spots)
            for to_core in range(2):
                to_shard = to * 4 + 2 * flip + to_core
                spread_to(chunk, cross_out.at[chunk, 1, to, to_core], 2 - level, near, to_shard)
                spread_to(chunk, cross_out.at[chunk, 0, to, to_core], 0, inst, to_shard)
            to_shard = to * 4 + 2 * level
            spread_to(chunk, level_out.at[chunk, 0, to], 1, after, to_shard)
            spread_to(chunk, level_out.at[chunk, 1, to], 2, before, to_shard + 1)
            return carry

        lax.fori_loop(0, spots, spread, 0)

    relay(0)
    spread_own(0)
    for chunk in range(1, CHUNKS):
        relay(chunk)

    some = pl.ds(0, n_inst - 1)
    waiting(part_got.at[some], part_send, part_recv).wait()
    row[...] = part_got[...].sum(axis=0)
    side_at, place = shard // SIDE, lax.rem(shard, SIDE)

    def share_row(step, carry):
        to = lax.rem(place + step, SIDE)
        copy(row, row_got.at[place], row_send, row_recv, inst, side_at * SIDE + to).start()
        return carry

    lax.fori_loop(1, SIDE, share_row, 0)
    row_got[place] = row[...]

    for chunk in range(CHUNKS):
        mix(chunk)
        spread_mixed(chunk)
        if chunk + 1 < CHUNKS:
            spread_own(chunk + 1)

    rotation = table[0] >> 1
    came = pl.ds(0, 5 * n_shard // 2 - 1)

    def held(chunk, owner):
        turn = (healthy[owner] - inst) & 3
        of_level = (owner >> 1) & 1
        same = jnp.where(turn == 0, 0, jnp.where(turn == 3, 1, jnp.where(turn == 1, 2, 1 + core)))
        beside = jnp.where(of_level == 1, 1, 3)
        other = jnp.where((turn == 0) | (turn == beside), 0, 2 - of_level)
        slot = jnp.where(of_level == level, same, other)
        return got[chunk][slot * n_shard + owner]

    def deal(chunk):
        waiting(got[chunk].at[came], spread_send.at[chunk], spread_recv.at[chunk]).wait_recv()

        def stage(new, carry):
            low = held(chunk, (new - rotation - 1) & (n_shard - 1))
            high = held(chunk, (new - rotation) & (n_shard - 1))
            lines = []
            for at in range(0, height, 2):
                lines += [low[:, at + 1:at + 2], high[:, at:at + 1]]
            staged[chunk, new] = jnp.concatenate(lines, axis=1)
            return carry

        lax.fori_loop(0, n_shard, stage, 0)
        place_there = final.at[:, chunk, inst, spot, level, core]

        def deal_to(recv_sem, to_inst, to_shard):
            copy(staged.at[chunk, to_shard], place_there, deal_send.at[chunk], recv_sem, to_inst, to_shard).start()

        def deal_cross(step, carry):
            to = lax.rem(spot + step, spots) * 4 + 2 * flip
            for to_core in range(2):
                deal_to(pass_recv.at[chunk, 0], inst, to + to_core)
                deal_to(pass_recv.at[chunk, 1], near, to + to_core)
            return carry

        passing = lax.rem(inst + 3 + 2 * core, n_inst)
        resting = lax.rem(inst + 1 + 2 * core, n_inst)

        def deal_passed(step, carry):
            to = lax.rem(spot + step, spots) * 4 + 2 * level
            for to_core in range(2):
                deal_to(pass_recv.at[chunk, 2 + core], passing, to + to_core)
            return carry

        def deal_rest(step, carry):
            to = lax.rem(spot + step, spots) * 4 + 2 * level
            for to_core in range(2):
                deal_to(deal_recv.at[chunk], resting, to + to_core)

            @pl.when(step > 0)
            def _():
                for to_core in range(2):
                    deal_to(deal_recv.at[chunk], inst, to + to_core)

            return carry

        lax.fori_loop(0, spots, deal_cross, 0)
        lax.fori_loop(0, spots, deal_passed, 0)
        lax.fori_loop(0, spots, deal_rest, 0)
        deal_to(deal_recv.at[chunk], inst, spot * 4 + 2 * level + 1 - core)
        final[:, chunk, inst, spot, level, core] = staged[chunk, shard]

    def passes(chunk):
        return (
            (final.at[:, chunk, inst, :, flip], near),
            (final.at[:, chunk, near, :, flip], far),
            (final.at[:, chunk, after, :, level, 0], before),
            (final.at[:, chunk, before, :, level, 1], after),
        )

    def passed(chunk):
        return (
            final.at[:, chunk, far, :, flip],
            final.at[:, chunk, across, :, flip],
            final.at[:, chunk, across, :, level, 0],
            final.at[:, chunk, across, :, level, 1],
        )

    def pass_on(chunk):
        for which, (there, to_inst) in enumerate(passes(chunk)):
            waiting(there, deal_send.at[chunk], pass_recv.at[chunk, which]).wait_recv()
            copy(there, there, far_send.at[chunk, which], far_recv.at[chunk, which], to_inst, shard).start()

    for chunk in range(CHUNKS):
        deal(chunk)
        if chunk == 0:
            few = pl.ds(0, SIDE - 1)
            waiting(row_got.at[few], row_send, row_recv).wait()
            total[...] = row_got[...].sum(axis=0)

            def share_total(step, carry):
                to = lax.rem(side_at + step, SIDE)
                copy(total, total_got.at[side_at], total_send, total_recv, inst, to * SIDE + place).start()
                return carry

            lax.fori_loop(1, SIDE, share_total, 0)
            total_got[side_at] = total[...]
    for chunk in range(CHUNKS):
        pass_on(chunk)

    waiting(total_got.at[pl.ds(0, SIDE - 1)], total_send, total_recv).wait()
    sums_out[...] = total_got[...].sum(axis=0)

    rest = pl.ds(0, n_shard - 1)
    for chunk in range(CHUNKS):
        waiting(got[chunk].at[rest], deal_send.at[chunk], deal_recv.at[chunk]).wait_recv()
        for which, there in enumerate(passed(chunk)):
            waiting(there, far_send.at[chunk, which], far_recv.at[chunk, which]).wait_recv()
        pltpu.make_async_copy(final.at[:, chunk], out.at[:, chunk], store_sem.at[chunk]).start()
    for chunk in range(CHUNKS):
        waiting(got[chunk].at[came], spread_send.at[chunk], spread_recv.at[chunk]).wait_send()
        waiting(got[chunk].at[came], deal_send.at[chunk], deal_recv.at[chunk]).wait_send()
        for _, target, which, _ in relays(chunk):
            waiting(target, relay_send.at[chunk, which], relay_recv.at[chunk, which]).wait_send()
        for which, there in enumerate(passed(chunk)):
            waiting(there, far_send.at[chunk, which], far_recv.at[chunk, which]).wait_send()
        pltpu.make_async_copy(final.at[:, chunk], out.at[:, chunk], store_sem.at[chunk]).wait()


def on_device(n_inst, n_shard, master_old, first_old, second_old, healthy, slice_table):
    rows, columns = master_old.shape[1:]
    spots = n_shard // 4
    pieces = (CHUNKS, n_inst, spots, 2, 2)
    arrays = [to_pieces(a, pieces) for a in (master_old, first_old, second_old)]
    tile = arrays[0].shape[5:]
    anywhere = pl.BlockSpec(memory_space=pl.ANY)
    vmem = pl.BlockSpec(memory_space=pltpu.VMEM)
    smem = pl.BlockSpec(memory_space=pltpu.SMEM)
    dma = pltpu.SemaphoreType.DMA

    def buffer(*shape):
        return pltpu.VMEM((*shape, *tile), jnp.float32)

    def sums(*shape):
        return pltpu.VMEM((*shape, 2, 128), jnp.float32)

    out, checks = pl.pallas_call(
        functools.partial(kernel, n_inst, n_shard),
        out_shape=(
            jax.ShapeDtypeStruct((KINDS, *pieces, *tile), jnp.float32),
            jax.ShapeDtypeStruct((2, 128), jnp.float32),
        ),
        in_specs=[smem, smem, anywhere, anywhere, anywhere],
        out_specs=(anywhere, vmem),
        scratch_shapes=[
            buffer(*pieces, KINDS),
            buffer(CHUNKS, 2, spots, 2, KINDS),
            buffer(CHUNKS, 2, spots, 2, KINDS),
            buffer(CHUNKS, 2, spots, KINDS),
            buffer(CHUNKS, 2, spots, KINDS),
            buffer(CHUNKS, n_shard, KINDS),
            buffer(KINDS, *pieces),
            sums(), sums(n_inst), sums(), sums(SIDE), sums(), sums(SIDE),
            dma((KINDS,)),
            dma((CHUNKS, 4)), dma((CHUNKS, 4)),
            dma((CHUNKS,)), dma((CHUNKS,)),
            dma((CHUNKS,)), dma((CHUNKS,)), dma((CHUNKS, 4)),
            dma((CHUNKS, 4)), dma((CHUNKS, 4)),
            dma, dma, dma, dma, dma, dma,
            dma((CHUNKS,)),
            *[buffer(3 * n_shard, KINDS) for _ in range(CHUNKS)],
        ],
        compiler_params=pltpu.CompilerParams(collective_id=0, has_side_effects=True),
    )(healthy, slice_table, *arrays)
    master, first_moment, second = (from_pieces(out[k], rows, columns) for k in range(KINDS))
    checksum = jnp.sum(checks, axis=1).reshape(1, 2) * (1.0 / (101.0 * 2.0 * columns))
    return master, first_moment, second, master.astype(jnp.bfloat16), checksum


def solution(mesh):
    per_slice = P("inst", "shard", None)
    return jax.shard_map(
        functools.partial(on_device, mesh.shape["inst"], mesh.shape["shard"]),
        mesh=mesh,
        in_specs=(per_slice, per_slice, per_slice, P(), P()),
        out_specs=(per_slice, per_slice, per_slice, per_slice, P("inst", None)),
        check_vma=False,
    )
```

time: 86.6 us -> 73.4 us (0.85)
  Pallas kernels: 81.2 us -> 68 us
    pallas_call x1, Pallas kernels: 81.2 us -> 68 us  [on_device(): pl.pallas_call(functools.partial(kernel, n_inst, n_shard), out_shape=(jax...]
where the time goes in v3:
time: 73.4 us; the launch traced here: 73.3 us
  Pallas kernels  68 us (93%)
  local copies, waits for them, and re-layouts  3.06 us (4%)
  other arithmetic  1.56 us (2%)
    pallas_call x1, Pallas kernels, on_device(): pl.pallas_call(functools.partial(kernel, n_inst, n_shard), out_shape=(jax...  68 us
    slice x1, local copies, waits for them, and re-layouts, on_device(): out[k]  3.06 us

profile of v3, /device:TPU:1, one launch (start us, length us, event | category | flops | bytes accessed | tf_op | source)
XLA Modules:
  0.0 73.3 jit_solution(9524546927967098888)
XLA Ops:
  0.6 68.0 %shard_map.92 = (f32[3,2,4,16,2,2,2,128]{7,6,5,4,3,2,1,0:T(2,128)}, f32[2,128]{1,0:T(2,128)}) custom-call(s32[64]{0:T(128)} %healthy.1, s32[128]{0:T(128)} %table.1, f32[2,4,16,2,2,2,128]{6,5,4,3,2,1,0:T(2,128)} %bitcast.34, f32[2,4,16,2,2,2,128]{6,5,4,3,2,1,0:T(2,128)} %bitcast.35, f32[2,4,16,2,2,2,128]{6,5,4,3,2,1,0:T(2,128)} %bitcast.36), custom_call_target="tpu_custom_call" | custom-call | tf_op jit(solution)/shard_map/pallas_call | solution.py:364
  68.6 0.0 copy-start.1
  68.6 3.1 %fusion = (f32[1,2,4,16,2,2,2,128]{7,6,5,4,3,2,1,0:T(2,128)}, f32[1,2,4,16,2,2,2,128]{7,6,5,4,3,2,1,0:T(2,128)}, f32[1,2,4,16,2,2,2,128]{7,6,5,4,3,2,1,0:T(2,128)S(1)}) fusion(f32[3,2,4,16,2,2,2,128]{7,6,5,4,3,2,1,0:T(2,128)} %get-tuple-element.7), kind=kLoop, calls=%fused_computation.1 | loop fusion | bytes 3145728 | tf_op jit(solution)/shard_map/slice | solution.py:392
  71.7 0.0 copy-start
  71.7 0.0 copy-done.1
  71.7 0.1 reduce_sum.9
  71.8 0.6 multiply_bitcast_fusion
  72.4 0.9 %convert_element_type.11 = bf16[1,2,65536]{2,1,0:T(2,128)(2,1)} convert(f32[1,2,65536]{2,1,0:T(2,128)S(1)} %bitcast.32) | non-fusion elementwise | flops 131072 | bytes 786432 | tf_op jit(solution)/shard_map/convert_element_type | solution.py:394
  73.3 0.0 copy-done
Async XLA Ops:
  68.6 3.1 %copy-start.1 = (f32[2,128]{1,0:T(2,128)S(1)}, f32[2,128]{1,0:T(2,128)}, u32[]{:S(2)}) copy-start(f32[2,128]{1,0:T(2,128)} %get-tuple-element.8) | copy-start | bytes 3076
  71.7 1.6 %copy-start = (f32[1,2,4,16,2,2,2,128]{7,6,5,4,3,2,1,0:T(2,128)}, f32[1,2,4,16,2,2,2,128]{7,6,5,4,3,2,1,0:T(2,128)S(1)}, u32[]{:S(2)}) copy-start(f32[1,2,4,16,2,2,2,128]{7,6,5,4,3,2,1,0:T(2,128)S(1)} %get-tuple-element.11) | copy-start | bytes 1572868

commit v4 on v3

--- a/solution.py
+++ b/solution.py
@@ -29,12 +29,12 @@
     return x - ((x * 10382) >> 20) * 101
 
 
-def kernel(n_inst, n_shard, healthy, table, master, first, second, out, sums_out,
-           own, cross_in, cross_out, level_in, level_out, staged, final,
+def kernel(n_inst, n_shard, healthy, table, master, first, second, final, sums_out,
+           own, cross_in, cross_out, level_in, level_out, staged,
            part, part_got, row, row_got, total, total_got,
            load_sem, relay_send, relay_recv, spread_send, spread_recv,
            deal_send, deal_recv, pass_recv, far_send, far_recv,
-           part_send, part_recv, row_send, row_recv, total_send, total_recv, store_sem, *got):
+           part_send, part_recv, row_send, row_recv, total_send, total_recv, *got):
     inst = lax.axis_index("inst")
     shard = lax.axis_index("shard")
     spots = n_shard // 4
@@ -333,7 +333,6 @@
         waiting(got[chunk].at[rest], deal_send.at[chunk], deal_recv.at[chunk]).wait_recv()
         for which, there in enumerate(passed(chunk)):
             waiting(there, far_send.at[chunk, which], far_recv.at[chunk, which]).wait_recv()
-        pltpu.make_async_copy(final.at[:, chunk], out.at[:, chunk], store_sem.at[chunk]).start()
     for chunk in range(CHUNKS):
         waiting(got[chunk].at[came], spread_send.at[chunk], spread_recv.at[chunk]).wait_send()
         waiting(got[chunk].at[came], deal_send.at[chunk], deal_recv.at[chunk]).wait_send()
@@ -341,7 +340,30 @@
             waiting(target, relay_send.at[chunk, which], relay_recv.at[chunk, which]).wait_send()
         for which, there in enumerate(passed(chunk)):
             waiting(there, far_send.at[chunk, which], far_recv.at[chunk, which]).wait_send()
-        pltpu.make_async_copy(final.at[:, chunk], out.at[:, chunk], store_sem.at[chunk]).wait()
+
+
+def finish(scale, state, checks, master, first, second, half, checksum, halved, sem):
+    stores = [
+        pltpu.make_async_copy(state.at[kind], target, sem.at[kind])
+        for kind, target in enumerate((master, first, second))
+    ]
+    for store in stores:
+        store.start()
+    tiles = state.shape[1]
+
+    def narrow(step, carry):
+        for tile in range(8):
+            at = pl.ds(pl.multiple_of((step * 8 + tile) * 128, 128), 128)
+            halved[0, :, at] = state[0, step * 8 + tile].astype(jnp.bfloat16)
+        return carry
+
+    lax.fori_loop(0, tiles // 8, narrow, 0)
+    last = pltpu.make_async_copy(halved, half, sem.at[KINDS])
+    last.start()
+    checksum[...] = checks[...].sum(axis=1).reshape(1, 2) * scale
+    for store in stores:
+        store.wait()
+    last.wait()
 
 
 def on_device(n_inst, n_shard, master_old, first_old, second_old, healthy, slice_table):
@@ -349,8 +371,11 @@
     spots = n_shard // 4
     pieces = (CHUNKS, n_inst, spots, 2, 2)
     arrays = [to_pieces(a, pieces) for a in (master_old, first_old, second_old)]
+    healthy, slice_table, *arrays = (
+        pltpu.with_memory_space_constraint(a, pltpu.HBM) for a in (healthy, slice_table, *arrays)
+    )
     tile = arrays[0].shape[5:]
-    anywhere = pl.BlockSpec(memory_space=pl.ANY)
+    anywhere = pl.BlockSpec(memory_space=pltpu.HBM)
     vmem = pl.BlockSpec(memory_space=pltpu.VMEM)
     smem = pl.BlockSpec(memory_space=pltpu.SMEM)
     dma = pltpu.SemaphoreType.DMA
@@ -368,7 +393,7 @@
             jax.ShapeDtypeStruct((2, 128), jnp.float32),
         ),
         in_specs=[smem, smem, anywhere, anywhere, anywhere],
-        out_specs=(anywhere, vmem),
+        out_specs=(vmem, vmem),
         scratch_shapes=[
             buffer(*pieces, KINDS),
             buffer(CHUNKS, 2, spots, 2, KINDS),
@@ -376,7 +401,6 @@
             buffer(CHUNKS, 2, spots, KINDS),
             buffer(CHUNKS, 2, spots, KINDS),
             buffer(CHUNKS, n_shard, KINDS),
-            buffer(KINDS, *pieces),
             sums(), sums(n_inst), sums(), sums(SIDE), sums(), sums(SIDE),
             dma((KINDS,)),
             dma((CHUNKS, 4)), dma((CHUNKS, 4)),
@@ -384,14 +408,24 @@
             dma((CHUNKS,)), dma((CHUNKS,)), dma((CHUNKS, 4)),
             dma((CHUNKS, 4)), dma((CHUNKS, 4)),
             dma, dma, dma, dma, dma, dma,
-            dma((CHUNKS,)),
             *[buffer(3 * n_shard, KINDS) for _ in range(CHUNKS)],
         ],
-        compiler_params=pltpu.CompilerParams(collective_id=0, has_side_effects=True),
+        compiler_params=pltpu.CompilerParams(collective_id=0, has_side_effects=True, vmem_limit_bytes=16 << 20),
     )(healthy, slice_table, *arrays)
-    master, first_moment, second = (from_pieces(out[k], rows, columns) for k in range(KINDS))
-    checksum = jnp.sum(checks, axis=1).reshape(1, 2) * (1.0 / (101.0 * 2.0 * columns))
-    return master, first_moment, second, master.astype(jnp.bfloat16), checksum
+    state = jax.ShapeDtypeStruct((columns // 128, rows, 128), jnp.float32)
+    *outs, half, checksum = pl.pallas_call(
+        functools.partial(finish, 1.0 / (101.0 * 2.0 * columns)),
+        out_shape=(
+            state, state, state,
+            jax.ShapeDtypeStruct((1, rows, columns), jnp.bfloat16),
+            jax.ShapeDtypeStruct((1, 2), jnp.float32),
+        ),
+        in_specs=[vmem, vmem],
+        out_specs=(*[pl.BlockSpec(memory_space=pltpu.HBM)] * 4, vmem),
+        scratch_shapes=[pltpu.VMEM((1, rows, columns), jnp.bfloat16), dma((KINDS + 1,))],
+        compiler_params=pltpu.CompilerParams(vmem_limit_bytes=4 << 20),
+    )(out.reshape(KINDS, columns // 128, rows, 128), checks)
+    return *(from_pieces(a, rows, columns) for a in outs), half, checksum
 
 
 def solution(mesh):

time: 73.4 us -> 69.3 us (0.944)
  local copies, waits for them, and re-layouts: 3.06 us -> 0 us
  other arithmetic: 1.56 us -> 0 us
    slice x1 -> x0, local copies, waits for them, and re-layouts: 3.06 us -> none  [on_device(): out[k]]
    pallas_call x0 -> x1, Pallas kernels: none -> 2.02 us  [on_device(): pl.pallas_call(functools.partial(finish, 1.0 / (101.0 * 2.0 * columns)),...]
    pallas_call x1, Pallas kernels: 68 us -> 66.5 us  [on_device(): pl.pallas_call(functools.partial(kernel, n_inst, n_shard), out_shape=(jax...]
    convert_element_type x1 -> x0, other arithmetic: 0.88 us -> none  [on_device(): return (master, first_moment, second, master.astype(jnp.bfloat16), checksum)]
where the time goes in v4:
time: 69.3 us; the launch traced here: 69.2 us
  Pallas kernels  68.5 us (99%)
    pallas_call x1, Pallas kernels, on_device(): pl.pallas_call(functools.partial(kernel, n_inst, n_shard), out_shape=(jax...  66.5 us
    pallas_call x1, Pallas kernels, on_device(): pl.pallas_call(functools.partial(finish, 1.0 / (101.0 * 2.0 * columns)),...  2.02 us

profile of v4, /device:TPU:1, one launch (start us, length us, event | category | flops | bytes accessed | tf_op | source)
XLA Modules:
  0.0 69.2 jit_solution(16079942277328980918)
XLA Ops:
  0.6 66.5 %shard_map.92 = (f32[3,2,4,16,2,2,2,128]{7,6,5,4,3,2,1,0:T(2,128)S(1)}, f32[2,128]{1,0:T(2,128)S(1)}) custom-call(s32[64]{0:T(128)} %healthy.1, s32[128]{0:T(128)} %table.1, f32[2,4,16,2,2,2,128]{6,5,4,3,2,1,0:T(2,128)} %bitcast.26, f32[2,4,16,2,2,2,128]{6,5,4,3,2,1,0:T(2,128)} %bitcast.27, f32[2,4,16,2,2,2,128]{6,5,4,3,2,1,0:T(2,128)} %bitcast.28), custom_call_target="tpu_custom_call" | custom-call | tf_op jit(solution)/shard_map/pallas_call | solution.py:389
  67.2 2.0 %shard_map.93 = (f32[512,2,128]{2,1,0:T(2,128)}, f32[512,2,128]{2,1,0:T(2,128)}, f32[512,2,128]{2,1,0:T(2,128)}, bf16[1,2,65536]{2,1,0:T(2,128)(2,1)}, f32[1,2]{1,0:T(1,128)}) custom-call(f32[3,512,2,128]{3,2,1,0:T(2,128)S(1)} %bitcast.25, f32[2,128]{1,0:T(2,128)S(1)} %get-tuple-element.13.checks), custom_call_target="tpu_custom_call" | custom-call | tf_op jit(solution)/shard_map/pallas_call | solution.py:416

commit v5 on v4

--- a/solution.py
+++ b/solution.py
@@ -29,10 +29,10 @@
     return x - ((x * 10382) >> 20) * 101
 
 
-def kernel(n_inst, n_shard, healthy, table, master, first, second, final, sums_out,
+def kernel(n_inst, n_shard, healthy_in, table_in, master, first, second, final, sums_out,
            own, cross_in, cross_out, level_in, level_out, staged,
            part, part_got, row, row_got, total, total_got,
-           load_sem, relay_send, relay_recv, spread_send, spread_recv,
+           healthy, table, load_sem, relay_send, relay_recv, spread_send, spread_recv,
            deal_send, deal_recv, pass_recv, far_send, far_recv,
            part_send, part_recv, row_send, row_recv, total_send, total_recv, *got):
     inst = lax.axis_index("inst")
@@ -64,6 +64,10 @@
         pltpu.make_async_copy(source, own.at[:, :, :, :, :, kind], load_sem.at[kind])
         for kind, source in enumerate((master, first, second))
     ]
+    loads += [
+        pltpu.make_async_copy(healthy_in, healthy, load_sem.at[KINDS]),
+        pltpu.make_async_copy(table_in, table, load_sem.at[KINDS + 1]),
+    ]
     for load in loads:
         load.start()
 
@@ -73,14 +77,16 @@
         pl.semaphore_signal(barrier, inc=1, device_id=(to_inst, to_shard), device_id_type=MESH)
 
     def greet_spot(step, carry):
-        to = lax.rem(spot + step, spots) * 4
+        to_y = lax.rem(spot // 4 + 6 - step // 4, 4)
+        to_x = lax.rem(lax.rem(spot, 4) + 6 - lax.rem(step, 4), 4)
+        to = (to_y * 4 + to_x) * 4
         for to_core in range(2):
             greet(near, to + 2 * flip + to_core)
-            greet(inst, to + 2 * flip + to_core)
             greet(after, to + 2 * level + to_core)
             greet(before, to + 2 * level + to_core)
-
-        @pl.when(step > 0)
+            greet(inst, to + 2 * flip + to_core)
+
+        @pl.when(to != spot * 4)
         def _():
             for to_core in range(2):
                 greet(inst, to + 2 * level + to_core)
@@ -357,7 +363,7 @@
             halved[0, :, at] = state[0, step * 8 + tile].astype(jnp.bfloat16)
         return carry
 
-    lax.fori_loop(0, tiles // 8, narrow, 0)
+    lax.fori_loop(0, tiles // 8, narrow, 0, unroll=4)
     last = pltpu.make_async_copy(halved, half, sem.at[KINDS])
     last.start()
     checksum[...] = checks[...].sum(axis=1).reshape(1, 2) * scale
@@ -377,7 +383,6 @@
     tile = arrays[0].shape[5:]
     anywhere = pl.BlockSpec(memory_space=pltpu.HBM)
     vmem = pl.BlockSpec(memory_space=pltpu.VMEM)
-    smem = pl.BlockSpec(memory_space=pltpu.SMEM)
     dma = pltpu.SemaphoreType.DMA
 
     def buffer(*shape):
@@ -392,7 +397,7 @@
             jax.ShapeDtypeStruct((KINDS, *pieces, *tile), jnp.float32),
             jax.ShapeDtypeStruct((2, 128), jnp.float32),
         ),
-        in_specs=[smem, smem, anywhere, anywhere, anywhere],
+        in_specs=[anywhere] * 5,
         out_specs=(vmem, vmem),
         scratch_shapes=[
             buffer(*pieces, KINDS),
@@ -402,7 +407,9 @@
             buffer(CHUNKS, 2, spots, KINDS),
             buffer(CHUNKS, n_shard, KINDS),
             sums(), sums(n_inst), sums(), sums(SIDE), sums(), sums(SIDE),
-            dma((KINDS,)),
+            pltpu.SMEM(healthy.shape, jnp.int32),
+            pltpu.SMEM(slice_table.shape, jnp.int32),
+            dma((KINDS + 2,)),
             dma((CHUNKS, 4)), dma((CHUNKS, 4)),
             dma((CHUNKS,)), dma((CHUNKS,)),
             dma((CHUNKS,)), dma((CHUNKS,)), dma((CHUNKS, 4)),

time: 69.3 us -> 67.5 us (0.974)
  Pallas kernels: 68.5 us -> 66.7 us
    pallas_call x1, Pallas kernels: 66.5 us -> 64.9 us  [on_device(): pl.pallas_call(functools.partial(kernel, n_inst, n_shard), out_shape=(jax...]
where the time goes in v5:
time: 67.5 us; the launch traced here: 67.3 us
  Pallas kernels  66.7 us (99%)
    pallas_call x1, Pallas kernels, on_device(): pl.pallas_call(functools.partial(kernel, n_inst, n_shard), out_shape=(jax...  64.9 us
    pallas_call x1, Pallas kernels, on_device(): pl.pallas_call(functools.partial(finish, 1.0 / (101.0 * 2.0 * columns)),...  1.77 us

profile of v5, /device:TPU:1, one launch (start us, length us, event | category | flops | bytes accessed | tf_op | source)
XLA Modules:
  0.0 67.3 jit_solution(4988764621465123406)
XLA Ops:
  0.6 64.9 %shard_map.92 = (f32[3,2,4,16,2,2,2,128]{7,6,5,4,3,2,1,0:T(2,128)S(1)}, f32[2,128]{1,0:T(2,128)S(1)}) custom-call(s32[64]{0:T(128)} %healthy_in.1, s32[128]{0:T(128)} %table_in.1, f32[2,4,16,2,2,2,128]{6,5,4,3,2,1,0:T(2,128)} %bitcast.26, f32[2,4,16,2,2,2,128]{6,5,4,3,2,1,0:T(2,128)} %bitcast.27, f32[2,4,16,2,2,2,128]{6,5,4,3,2,1,0:T(2,128)} %bitcast.28), custom_call_target="tpu_custom_call" | custom-call | tf_op jit(solution)/shard_map/pallas_call | solution.py:394
  65.5 1.8 %shard_map.93 = (f32[512,2,128]{2,1,0:T(2,128)}, f32[512,2,128]{2,1,0:T(2,128)}, f32[512,2,128]{2,1,0:T(2,128)}, bf16[1,2,65536]{2,1,0:T(2,128)(2,1)}, f32[1,2]{1,0:T(1,128)}) custom-call(f32[3,512,2,128]{3,2,1,0:T(2,128)S(1)} %bitcast.25, f32[2,128]{1,0:T(2,128)S(1)} %get-tuple-element.13.checks), custom_call_target="tpu_custom_call" | custom-call | tf_op jit(solution)/shard_map/pallas_call | solution.py:423

commit v6 on v5

--- a/solution.py
+++ b/solution.py
@@ -47,6 +47,11 @@
     near = lax.rem(inst + 3 + 2 * level, n_inst)
     far = lax.rem(inst + 1 + 2 * level, n_inst)
 
+    def far_first(step):
+        to_y = lax.rem(spot // 4 + 6 - step // 4, 4)
+        to_x = lax.rem(lax.rem(spot, 4) + 6 - lax.rem(step, 4), 4)
+        return to_y * 4 + to_x
+
     def copy(source, target, send_sem, recv_sem, to_inst, to_shard):
         return pltpu.make_async_remote_copy(
             src_ref=source,
@@ -193,7 +198,7 @@
 
     def spread_mixed(chunk):
         def spread(step, carry):
-            to = lax.rem(spot + step, spots)
+            to = far_first(step)
             for to_core in range(2):
                 to_shard = to * 4 + 2 * flip + to_core
                 spread_to(chunk, cross_out.at[chunk, 1, to, to_core], 2 - level, near, to_shard)
@@ -260,7 +265,7 @@
             copy(staged.at[chunk, to_shard], place_there, deal_send.at[chunk], recv_sem, to_inst, to_shard).start()
 
         def deal_cross(step, carry):
-            to = lax.rem(spot + step, spots) * 4 + 2 * flip
+            to = far_first(step) * 4 + 2 * flip
             for to_core in range(2):
                 deal_to(pass_recv.at[chunk, 0], inst, to + to_core)
                 deal_to(pass_recv.at[chunk, 1], near, to + to_core)
@@ -270,7 +275,7 @@
         resting = lax.rem(inst + 1 + 2 * core, n_inst)
 
         def deal_passed(step, carry):
-            to = lax.rem(spot + step, spots) * 4 + 2 * level
+            to = far_first(step) * 4 + 2 * level
             for to_core in range(2):
                 deal_to(pass_recv.at[chunk, 2 + core], passing, to + to_core)
             return carry

time: 67.5 us -> 67.9 us (level)
  no operation moved by 1% of the time
where the time goes in v6:
time: 67.9 us; the launch traced here: 67.8 us
  Pallas kernels  67.2 us (99%)
    pallas_call x1, Pallas kernels, on_device(): pl.pallas_call(functools.partial(kernel, n_inst, n_shard), out_shape=(jax...  65.4 us
    pallas_call x1, Pallas kernels, on_device(): pl.pallas_call(functools.partial(finish, 1.0 / (101.0 * 2.0 * columns)),...  1.77 us

profile of v6, /device:TPU:1, one launch (start us, length us, event | category | flops | bytes accessed | tf_op | source)
XLA Modules:
  0.0 67.8 jit_solution(2012954665641000365)
XLA Ops:
  0.6 65.4 %shard_map.92 = (f32[3,2,4,16,2,2,2,128]{7,6,5,4,3,2,1,0:T(2,128)S(1)}, f32[2,128]{1,0:T(2,128)S(1)}) custom-call(s32[64]{0:T(128)} %healthy_in.1, s32[128]{0:T(128)} %table_in.1, f32[2,4,16,2,2,2,128]{6,5,4,3,2,1,0:T(2,128)} %bitcast.26, f32[2,4,16,2,2,2,128]{6,5,4,3,2,1,0:T(2,128)} %bitcast.27, f32[2,4,16,2,2,2,128]{6,5,4,3,2,1,0:T(2,128)} %bitcast.28), custom_call_target="tpu_custom_call" | custom-call | tf_op jit(solution)/shard_map/pallas_call | solution.py:399
  66.1 1.8 %shard_map.93 = (f32[512,2,128]{2,1,0:T(2,128)}, f32[512,2,128]{2,1,0:T(2,128)}, f32[512,2,128]{2,1,0:T(2,128)}, bf16[1,2,65536]{2,1,0:T(2,128)(2,1)}, f32[1,2]{1,0:T(1,128)}) custom-call(f32[3,512,2,128]{3,2,1,0:T(2,128)S(1)} %bitcast.25, f32[2,128]{1,0:T(2,128)S(1)} %get-tuple-element.13.checks), custom_call_target="tpu_custom_call" | custom-call | tf_op jit(solution)/shard_map/pallas_call | solution.py:428
